TPU v7x, 256 devices: a whole 4x4x8 slice. The times are simulated.
256 devices in a mesh: expert: 8 (over x, core), shard: 32 (over z, y).
Axes of the slice: x: 4, y: 4, z: 8, core: 2. Of those that a mesh axis runs over, the one named last changes fastest.
Arguments:
- w_gate: float32 [64, 2048, 1408], P('expert', 'shard'), may hold values from -0.25 to 0.25
- w_up: float32 [64, 2048, 1408], P('expert', 'shard'), may hold values from -0.25 to 0.25
- router_weight: float32 [2048, 64], P('shard', 'expert'), may hold values from -0.125 to 0.125
- router_gain: float32 [2048], P('shard'), may hold values from 0.25 to 1.75
Outputs:
- serve_gate: bfloat16 [64, 2048, 1408], P('expert', None, 'shard')
- serve_up: bfloat16 [64, 2048, 1408], P('expert', None, 'shard')
- scale_gate: float32 [64, 1408], P('expert', 'shard')
- scale_up: float32 [64, 1408], P('expert', 'shard')
- serve_router: bfloat16 [2048, 64], replicated
All inputs are finite; a program needn't handle non-finite values. Where the computation divides by a largest or mean magnitude, that divisor is 1e-20 or more.
Results may differ from a plain program's by a relative error of at most 0.001.
Values may be sent and summed in bfloat16 or wider, within the bound.
No kernel may reach another device: no remote copies, remote signals or barrier semaphores. Data moves between devices by JAX's collectives and lax.ppermute only.
A program may use at most 64 MiB of HBM per device.

v0:
```python
import jax
import jax.numpy as jnp
from jax import lax
from jax.sharding import PartitionSpec as P

D_MODEL = 2048


def split_up(shard, dim, size):
    shape = shard.shape
    parts = shard.reshape(*shape[:dim], size, shape[dim] // size, *shape[dim + 1 :])
    return jnp.moveaxis(parts, dim, 0)


def sent_and_summed(shard, axis, dim):
    parts = split_up(shard, dim, lax.axis_size(axis))
    arrived = lax.all_to_all(parts, axis, split_axis=0, concat_axis=0, tiled=True)
    return arrived.sum(axis=0)


def rows_for(lines, size):
    spare = -lines.shape[0] % size
    if not spare:
        return lines
    return jnp.concatenate([lines, jnp.zeros((spare, *lines.shape[1:]), lines.dtype)])


def in_order(parts, dim):
    shape = list(parts.shape[1:])
    shape[dim] *= parts.shape[0]
    return jnp.moveaxis(parts, 0, dim).reshape(shape)


def from_everyone(shard, axis):
    size = lax.axis_size(axis)
    return lax.all_to_all(
        jnp.broadcast_to(shard[None], (size, *shard.shape)), axis, 0, 0, tiled=True
    )


def gathered_copies(shard, axis, dim):
    return in_order(from_everyone(shard, axis), dim)


def total_of(shard, axes):
    own = sent_and_summed(rows_for(shard, lax.axis_size(axes)), axes, 0)
    whole = gathered_copies(own, axes, 0)
    return whole[: len(shard)].reshape(shard.shape)


def packed_total(arrays, axis):
    ends = [0]
    for a in arrays:
        ends.append(ends[-1] + a.size)
    total = total_of(jnp.concatenate([a.ravel() for a in arrays]), axis)
    return tuple((total[b:e].reshape(a.shape) for a, b, e in zip(arrays, ends, ends[1:])))


def in_one_piece(arrays, axis, split_dim, concat_dim, along):
    ends, at = ([], 0)
    for a in arrays[:-1]:
        at += a.shape[along]
        ends.append(at)
    both = jnp.concatenate(arrays, axis=along)
    return tuple(
        jnp.split(
            lax.all_to_all(both, axis, split_axis=split_dim, concat_axis=concat_dim, tiled=True),
            ends,
            axis=along,
        )
    )


def on_device(w_gate, w_up, router_weight, router_gain):
    total_gate, total_up = packed_total(
        (jnp.sum(jnp.abs(w_gate), axis=1), jnp.sum(jnp.abs(w_up), axis=1)), "shard"
    )
    scale_gate = total_gate / D_MODEL
    scale_up = total_up / D_MODEL
    narrow_gate, narrow_up = (
        (w_gate / jnp.expand_dims(scale_gate, 1)).astype(jnp.bfloat16),
        (w_up / jnp.expand_dims(scale_up, 1)).astype(jnp.bfloat16),
    )
    serve_gate, serve_up = in_one_piece((narrow_gate, narrow_up), "shard", 2, 1, 0)
    scale_gate = lax.dynamic_slice_in_dim(
        scale_gate, lax.axis_index("shard") * serve_gate.shape[2], serve_gate.shape[2], axis=1
    )
    scale_up = lax.dynamic_slice_in_dim(
        scale_up, lax.axis_index("shard") * serve_up.shape[2], serve_up.shape[2], axis=1
    )
    part_router = (router_weight * router_gain[:, None]).astype(jnp.bfloat16)
    row_router = gathered_copies(part_router, "shard", 0)
    serve_router = gathered_copies(row_router, "expert", 1)
    return (serve_gate, serve_up, scale_gate, scale_up, serve_router)


def solution(mesh):
    placed = (
        P("expert", "shard", None),
        P("expert", "shard", None),
        P("shard", "expert"),
        P("shard"),
    )
    return jax.shard_map(
        on_device,
        mesh=mesh,
        in_specs=placed,
        out_specs=(
            P("expert", None, "shard"),
            P("expert", None, "shard"),
            P("expert", "shard"),
            P("expert", "shard"),
            P(),
        ),
        check_vma=False,
    )
```

profile of v0, /device:TPU:8, one launch (start us, length us, event | category | flops | bytes accessed | tf_op | source)
XLA Modules:
  0.0 178.4 jit_solution(17516819587197205589)
XLA Ops:
  0.7 2.2 %abs_reduce_fusion.1 = f32[8,1408]{1,0:T(8,128)S(1)} fusion(f32[8,64,1408]{2,1,0:T(8,128)} %param.4), kind=kLoop, calls=%fused_computation.4 | loop fusion | flops 1430528 | bytes 2928640 | tf_op jit(solution)/shard_map/reduce_sum | solution.py:76
  2.9 2.3 %abs_reduce_fusion = f32[8,1408]{1,0:T(8,128)S(1)} fusion(f32[8,64,1408]{2,1,0:T(8,128)} %param.5), kind=kLoop, calls=%fused_computation.3 | loop fusion | flops 1430528 | bytes 2928640 | tf_op jit(solution)/shard_map/reduce_sum | solution.py:76
  5.3 0.7 all_to_all.27
  6.0 11.7 %all-to-all-start = ((f32[32,1,704]{2,1,0:T(1,128)}), f32[32,1,704]{2,1,0:T(1,128)S(1)}, u32[]{:S(2)}, u32[]{:S(2)}) async-start(f32[32,1,704]{2,1,0:T(1,128)} %all_to_all.27), calls=%async_computation | async-start | bytes 196608 | tf_op jit(solution)/shard_map/all_to_all | solution.py:17
  17.8 0.7 reshape.65
  18.5 8.0 %all-to-all-done = f32[32,1,704]{2,1,0:T(1,128)S(1)} async-done(((f32[32,1,704]{2,1,0:T(1,128)}), f32[32,1,704]{2,1,0:T(1,128)S(1)}, u32[]{:S(2)}, u32[]{:S(2)}) %all-to-all-start) | async-done | bytes 90144 | tf_op jit(solution)/shard_map/all_to_all | solution.py:17
  26.5 5.2 %all-to-all-start.3 = ((bf16[32,2,256]{2,1,0:T(2,128)(2,1)}), bf16[32,2,256]{2,1,0:T(2,128)(2,1)S(1)}, u32[]{:S(2)}, u32[]{:S(2)}) async-start(bf16[32,2,256]{2,1,0:T(2,128)(2,1)} %reshape.65), calls=%async_computation.3 | async-start | bytes 65536 | tf_op jit(solution)/shard_map/all_to_all | solution.py:36
  31.8 8.7 %all-to-all-done.3 = bf16[32,2,256]{2,1,0:T(2,128)(2,1)S(1)} async-done(((bf16[32,2,256]{2,1,0:T(2,128)(2,1)}), bf16[32,2,256]{2,1,0:T(2,128)(2,1)S(1)}, u32[]{:S(2)}, u32[]{:S(2)}) %all-to-all-start.3) | async-done | bytes 32800 | tf_op jit(solution)/shard_map/all_to_all | solution.py:36
  41.1 4.9 %all-to-all-start.1 = ((f32[32,1,704]{2,1,0:T(1,128)}), f32[32,1,704]{2,1,0:T(1,128)S(1)}, u32[]{:S(2)}, u32[]{:S(2)}) async-start(f32[32,1,704]{2,1,0:T(1,128)} %broadcast_in_dim.8), calls=%async_computation.1 | async-start | bytes 196608 | tf_op jit(solution)/shard_map/all_to_all | solution.py:36
  46.0 4.1 %copy.27 = f32[8,64,1408]{1,0,2:T(8,128)} copy(f32[8,64,1408]{2,1,0:T(8,128)S(1)} %copy-done) | data formatting | bytes 5767168 | tf_op args[0]
  50.1 5.4 %copy.29 = f32[8,64,1408]{1,0,2:T(8,128)} copy(f32[8,64,1408]{2,1,0:T(8,128)} %param.5) | data formatting | bytes 5767168 | tf_op args[1]
  55.8 0.7 broadcast_in_dim.11
  56.5 4.3 %all-to-all-start.4 = ((bf16[8,2048,8]{1,2,0:T(8,128)(2,1)}), bf16[8,2048,8]{1,2,0:T(8,128)(2,1)S(1)}, u32[]{:S(2)}, u32[]{:S(2)}) async-start(bf16[8,2048,8]{1,2,0:T(8,128)(2,1)} %broadcast_in_dim.11), calls=%async_computation.4 | async-start | bytes 524288 | tf_op jit(solution)/shard_map/all_to_all | solution.py:36
  61.8 6.4 %divide_convert_fusion = (bf16[8,64,1408]{1,0,2:T(8,128)(2,1)S(1)}, bf16[8,64,1408]{1,0,2:T(8,128)(2,1)S(1)}) fusion(f32[8,64,1408]{1,0,2:T(8,128)} %copy.29, f32[8,1408]{0,1:T(8,128)S(1)} %copy.28, f32[8,64,1408]{1,0,2:T(8,128)} %copy.27, f32[8,1408]{0,1:T(8,128)S(1)} %copy.26), kind=kLoop, calls=%fused_computation.1 | loop fusion | flops 2883584 | bytes 8740864 | tf_op jit(solution)/shard_map/convert_element_type | solution.py:82
  68.2 3.5 %fusion.3 = bf16[1408,16,64]{2,1,0:T(8,128)(2,1)} fusion(bf16[8,64,1408]{1,0,2:T(8,128)(2,1)S(1)} %get-tuple-element.9, bf16[8,64,1408]{1,0,2:T(8,128)(2,1)S(1)} %get-tuple-element.10), kind=kLoop, calls=%fused_computation.14 | loop fusion | flops 5767168 | bytes 5767168
  71.7 8.5 %reshape.63 = bf16[32,2,22528]{2,1,0:T(2,128)(2,1)} reshape(bf16[1408,16,64]{2,1,0:T(8,128)(2,1)} %fusion.3) | data formatting | bytes 5767168
  80.2 9.9 %all-to-all-start.2 = ((bf16[32,2,22528]{2,1,0:T(2,128)(2,1)}), bf16[32,2,22528]{2,1,0:T(2,128)(2,1)S(1)}, u32[]{:S(2)}, u32[]{:S(2)}) async-start(bf16[32,2,22528]{2,1,0:T(2,128)(2,1)} %reshape.63), calls=%async_computation.2 | async-start | bytes 5767168 | tf_op jit(solution)/shard_map/all_to_all | solution.py:67
  90.7 65.9 %all-to-all-done.2 = bf16[32,2,22528]{2,1,0:T(2,128)(2,1)S(1)} async-done(((bf16[32,2,22528]{2,1,0:T(2,128)(2,1)}), bf16[32,2,22528]{2,1,0:T(2,128)(2,1)S(1)}, u32[]{:S(2)}, u32[]{:S(2)}) %all-to-all-start.2) | async-done | bytes 2883616 | tf_op jit(solution)/shard_map/all_to_all | solution.py:67
  156.7 5.9 %reshape.64 = bf16[1408,16,64]{2,1,0:T(8,128)(2,1)} reshape(bf16[32,2,22528]{2,1,0:T(2,128)(2,1)S(1)} %all-to-all-done.2) | data formatting | bytes 5767168
  162.6 4.7 %fusion.2 = (bf16[8,32,64,44]{2,0,3,1:T(8,128)(2,1)}, bf16[8,32,64,44]{2,0,3,1:T(8,128)(2,1)S(1)}) fusion(bf16[16,32,64,44]{2,0,3,1:T(8,128)(2,1)} %bitcast.22), kind=kLoop, calls=%fused_computation.13 | loop fusion | bytes 5767168 | tf_op jit(solution)/shard_map/split | solution.py:66
  167.2 1.1 copy.30
  168.4 3.2 %split.11 = bf16[8,2048,44]{1,0,2:T(8,128)(2,1)} reshape(bf16[8,32,64,44]{2,1,0,3:T(8,128)(2,1)S(1)} %copy.30) | data formatting | bytes 2883584 | tf_op jit(solution)/shard_map/split | solution.py:66
  171.6 2.9 %copy.31 = bf16[8,32,64,44]{2,1,0,3:T(8,128)(2,1)S(1)} copy(bf16[8,32,64,44]{2,0,3,1:T(8,128)(2,1)} %get-tuple-element.7) | data formatting | bytes 2883584 | tf_op jit(solution)/shard_map/split | solution.py:66
  174.5 3.2 %split.13 = bf16[8,2048,44]{1,0,2:T(8,128)(2,1)} reshape(bf16[8,32,64,44]{2,1,0,3:T(8,128)(2,1)S(1)} %copy.31) | data formatting | bytes 2883584 | tf_op jit(solution)/shard_map/split | solution.py:66
  (25 shorter events, 3.5 us)
Async XLA Ops:
  0.6 17.1 %copy-start.1 = (f32[64,8]{0,1:T(8,128)S(1)}, f32[64,8]{0,1:T(8,128)}, u32[]{:S(2)}) copy-start(f32[64,8]{0,1:T(8,128)} %param.6) | copy-start | bytes 6148
  0.6 17.1 %copy-start.2 = (f32[64]{0:T(128)S(1)}, f32[64]{0:T(128)}, u32[]{:S(2)}) copy-start(f32[64]{0:T(128)} %param.7) | copy-start | bytes 772
  2.8 43.2 %copy-start = (f32[8,64,1408]{2,1,0:T(8,128)S(1)}, f32[8,64,1408]{2,1,0:T(8,128)}, u32[]{:S(2)}) copy-start(f32[8,64,1408]{2,1,0:T(8,128)} %param.4) | copy-start | bytes 8650756
  6.0 20.5 %all-to-all-start = ((f32[32,1,704]{2,1,0:T(1,128)}), f32[32,1,704]{2,1,0:T(1,128)S(1)}, u32[]{:S(2)}, u32[]{:S(2)}) async-start(f32[32,1,704]{2,1,0:T(1,128)} %all_to_all.27), calls=%async_computation | async-start | bytes 196608 | tf_op jit(solution)/shard_map/all_to_all | solution.py:17
  26.5 13.9 %all-to-all-start.3 = ((bf16[32,2,256]{2,1,0:T(2,128)(2,1)}), bf16[32,2,256]{2,1,0:T(2,128)(2,1)S(1)}, u32[]{:S(2)}, u32[]{:S(2)}) async-start(bf16[32,2,256]{2,1,0:T(2,128)(2,1)} %reshape.65), calls=%async_computation.3 | async-start | bytes 65536 | tf_op jit(solution)/shard_map/all_to_all | solution.py:36
  41.1 14.7 %all-to-all-start.1 = ((f32[32,1,704]{2,1,0:T(1,128)}), f32[32,1,704]{2,1,0:T(1,128)S(1)}, u32[]{:S(2)}, u32[]{:S(2)}) async-start(f32[32,1,704]{2,1,0:T(1,128)} %broadcast_in_dim.8), calls=%async_computation.1 | async-start | bytes 196608 | tf_op jit(solution)/shard_map/all_to_all | solution.py:36
  56.5 23.6 %all-to-all-start.4 = ((bf16[8,2048,8]{1,2,0:T(8,128)(2,1)}), bf16[8,2048,8]{1,2,0:T(8,128)(2,1)S(1)}, u32[]{:S(2)}, u32[]{:S(2)}) async-start(bf16[8,2048,8]{1,2,0:T(8,128)(2,1)} %broadcast_in_dim.11), calls=%async_computation.4 | async-start | bytes 524288 | tf_op jit(solution)/shard_map/all_to_all | solution.py:36
  80.2 76.5 %all-to-all-start.2 = ((bf16[32,2,22528]{2,1,0:T(2,128)(2,1)}), bf16[32,2,22528]{2,1,0:T(2,128)(2,1)S(1)}, u32[]{:S(2)}, u32[]{:S(2)}) async-start(bf16[32,2,22528]{2,1,0:T(2,128)(2,1)} %reshape.63), calls=%async_computation.2 | async-start | bytes 5767168 | tf_op jit(solution)/shard_map/all_to_all | solution.py:67
where the time goes:
time: 181 us; the launch traced here: 178 us
  waiting for transfers between devices  82.6 us (46%)
  local copies, waits for them, and re-layouts  44.4 us (25%)
  starting transfers between devices  36 us (20%)
  other arithmetic  14.7 us (8%)
    all_to_all x1, waiting for transfers between devices, in_one_piece(): lax.all_to_all(both, axis, split_axis=split_dim, concat_axis=concat_dim,...  65.9 us
    unnamed x14, local copies, waits for them, and re-layouts  25.5 us
    split x5, local copies, waits for them, and re-layouts, in_one_piece(): jnp.split(lax.all_to_all(both, axis, split_axis=split_dim, concat_axis=co...  15.1 us
    all_to_all x3, starting transfers between devices, from_everyone(): lax.all_to_all(jnp.broadcast_to(shard[None], (size, *shard.shape)), axis,...  14.4 us
    all_to_all x1, starting transfers between devices, sent_and_summed(): lax.all_to_all(parts, axis, split_axis=0, concat_axis=0, tiled=True)  11.7 us
    all_to_all x1, starting transfers between devices, in_one_piece(): lax.all_to_all(both, axis, split_axis=split_dim, concat_axis=concat_dim,...  9.88 us
    all_to_all x3, waiting for transfers between devices, from_everyone(): lax.all_to_all(jnp.broadcast_to(shard[None], (size, *shard.shape)), axis,...  8.66 us
    all_to_all x1, waiting for transfers between devices, sent_and_summed(): lax.all_to_all(parts, axis, split_axis=0, concat_axis=0, tiled=True)  7.99 us
  transfers between devices with their start and end apart: 5, of which 3 were waited for; matrix products, arithmetic and copies ran while one was open for 17% of the time, Pallas kernels for 0%

commit v1 on v0

v1 whole, which is shorter than its diff:
```python
import functools

import jax
import jax.numpy as jnp
from jax import lax
from jax.experimental import pallas as pl
from jax.experimental.pallas import tpu as pltpu
from jax.sharding import PartitionSpec as P

D_MODEL = 2048
LANES = 128
HALF = LANES // 2
EXPERT_ROWS = 8


def sums_kernel(own, gate_ref, up_ref, router_ref, gain_ref, out_ref, gate_sums, up_sums):
    step = pl.program_id(0)
    gate_sums[pl.ds(step, 1), :] = jnp.sum(jnp.abs(gate_ref[0]), axis=0, keepdims=True)
    up_sums[pl.ds(step, 1), :] = jnp.sum(jnp.abs(up_ref[0]), axis=0, keepdims=True)

    @pl.when(step == pl.num_programs(0) - 1)
    def _():
        router = (router_ref[...] * gain_ref[...]).astype(jnp.bfloat16).astype(jnp.float32)
        router = jnp.concatenate([router, jnp.zeros_like(router)], axis=1)
        spare = jnp.zeros((EXPERT_ROWS, HALF - own), jnp.float32)
        for d in range(out_ref.shape[0]):
            columns = slice(d * own, (d + 1) * own)
            out_ref[d, 0] = jnp.concatenate(
                [gate_sums[:, columns], spare, up_sums[:, columns], spare], axis=1
            )
            out_ref[d, 1] = router


def column_sums(w_gate, w_up, router_weight, router_gain, size):
    experts, rows, width = w_gate.shape
    whole = lambda a: pl.BlockSpec(a.shape, lambda e: (0,) * a.ndim)
    router = router_weight.T
    gain = router_gain[None]
    expert = pl.BlockSpec((1, rows, width), lambda e: (e, 0, 0))
    shape = (size, 2, EXPERT_ROWS, LANES)
    return pl.pallas_call(
        functools.partial(sums_kernel, width // size),
        grid=(experts,),
        in_specs=[expert, expert, whole(router), whole(gain)],
        out_specs=pl.BlockSpec(shape, lambda e: (0, 0, 0, 0)),
        out_shape=jax.ShapeDtypeStruct(shape, jnp.float32),
        scratch_shapes=[pltpu.VMEM((experts, width), jnp.float32)] * 2,
        cost_estimate=pl.CostEstimate(flops=4_000_000, bytes_accessed=6_000_000, transcendentals=0),
        name="column_sums",
    )(w_gate, w_up, router, gain)


def turned_kernel(gate_ref, up_ref, out_ref):
    for e in range(gate_ref.shape[0]):
        both = jnp.concatenate([gate_ref[e], up_ref[e]], axis=0)
        out_ref[:, e, :] = both.T


def turned(w_gate, w_up):
    experts, rows, width = w_gate.shape
    block = pl.BlockSpec((experts, rows, LANES), lambda c: (0, 0, c))
    return pl.pallas_call(
        turned_kernel,
        grid=(width // LANES,),
        in_specs=[block, block],
        out_specs=pl.BlockSpec((LANES, experts, LANES), lambda c: (c, 0, 0)),
        out_shape=jax.ShapeDtypeStruct((width, experts, LANES), jnp.float32),
        cost_estimate=pl.CostEstimate(flops=8_000_000, bytes_accessed=12_000_000, transcendentals=0),
        name="turned",
    )(w_gate, w_up)


def scaled_kernel(own, turned_ref, scale_ref, out_ref):
    left = lax.broadcasted_iota(jnp.int32, (EXPERT_ROWS, LANES), 1) < HALF
    for d in range(scale_ref.shape[0]):
        inverse = 1.0 / scale_ref[d]
        for j in range(own):
            factor = jnp.where(left, inverse[:, j : j + 1], inverse[:, HALF + j : HALF + j + 1])
            out_ref[d, j] = (turned_ref[d * own + j] * factor).astype(jnp.bfloat16)


def scaled(tall, scales):
    width, experts, lanes = tall.shape
    size = scales.shape[0]
    own = width // size
    part = 4
    return pl.pallas_call(
        functools.partial(scaled_kernel, own),
        grid=(size // part,),
        in_specs=[
            pl.BlockSpec((part * own, experts, lanes), lambda c: (c, 0, 0)),
            pl.BlockSpec((part, EXPERT_ROWS, LANES), lambda c: (c, 0, 0)),
        ],
        out_specs=pl.BlockSpec((part, own, experts, lanes), lambda c: (c, 0, 0, 0)),
        out_shape=jax.ShapeDtypeStruct((size, own, experts, lanes), jnp.bfloat16),
        cost_estimate=pl.CostEstimate(flops=8_000_000, bytes_accessed=9_000_000, transcendentals=0),
        name="scaled",
    )(tall, scales)


def placed_kernel(arrived_ref, gate_ref, up_ref):
    for p in range(arrived_ref.shape[0] // 2):
        first, second = arrived_ref[2 * p], arrived_ref[2 * p + 1]
        lanes = slice(p * LANES, (p + 1) * LANES)
        gate_ref[:, :, lanes] = jnp.concatenate([first[..., :HALF], second[..., :HALF]], axis=-1)
        up_ref[:, :, lanes] = jnp.concatenate([first[..., HALF:], second[..., HALF:]], axis=-1)


def placed(arrived):
    size, own, experts, lanes = arrived.shape
    part = 11
    rows = size * HALF
    out = jax.ShapeDtypeStruct((own, experts, rows), jnp.bfloat16)
    return pl.pallas_call(
        placed_kernel,
        grid=(own // part,),
        in_specs=[pl.BlockSpec((size, part, experts, lanes), lambda c: (0, c, 0, 0))],
        out_specs=[pl.BlockSpec((part, experts, rows), lambda c: (c, 0, 0))] * 2,
        out_shape=[out, out],
        cost_estimate=pl.CostEstimate(flops=4_000_000, bytes_accessed=6_000_000, transcendentals=0),
        name="placed",
    )(arrived)


def exchanged(parts, axis):
    return lax.all_to_all(parts, axis, split_axis=0, concat_axis=0, tiled=True)


def on_device(w_gate, w_up, router_weight, router_gain):
    size = lax.axis_size("shard")
    own = w_gate.shape[2] // size
    sums = column_sums(w_gate, w_up, router_weight, router_gain, size)
    arrived = exchanged(sums, "shard")
    scale = jnp.sum(arrived[:, 0], axis=0) / D_MODEL
    scales = exchanged(jnp.broadcast_to(scale[None], (size, *scale.shape)), "shard")
    tall = turned(w_gate, w_up)
    serve = exchanged(scaled(tall, scales), "shard")
    serve_gate, serve_up = placed(serve)
    rows = arrived[:, 1, :, :HALF].astype(jnp.bfloat16)
    rows = jnp.transpose(rows, (1, 0, 2)).reshape(EXPERT_ROWS, -1)
    router = lax.all_gather(rows, "expert", axis=0, tiled=True)
    return (
        jnp.transpose(serve_gate, (1, 2, 0)),
        jnp.transpose(serve_up, (1, 2, 0)),
        scale[:, :own],
        scale[:, HALF : HALF + own],
        router.T,
    )


def solution(mesh):
    placed_in = (
        P("expert", "shard", None),
        P("expert", "shard", None),
        P("shard", "expert"),
        P("shard"),
    )
    return jax.shard_map(
        on_device,
        mesh=mesh,
        in_specs=placed_in,
        out_specs=(
            P("expert", None, "shard"),
            P("expert", None, "shard"),
            P("expert", "shard"),
            P("expert", "shard"),
            P(),
        ),
        check_vma=False,
    )
```

time: 181 us -> 140 us (0.77)
  local copies, waits for them, and re-layouts: 44.4 us -> 4.42 us
  blocking collectives: 0 us -> 36.1 us
  waiting for transfers between devices: 82.6 us -> 52 us
  Pallas kernels: 0 us -> 30.4 us
  starting transfers between devices: 36 us -> 15.3 us
  other arithmetic: 14.7 us -> 0.04 us
    all_to_all x5 -> x2, waiting for transfers between devices: 82.6 us -> 52 us  [exchanged(): return lax.all_to_all(parts, axis, split_axis=0, concat_axis=0, tiled=True)]
    pallas_call x0 -> x4, Pallas kernels: none -> 30.4 us  [the longest x1 10.3 us: turned(): pl.pallas_call(turned_kernel, grid=(width // LANES,), in_specs=[block, bl...]
    all_to_all x0 -> x1, blocking collectives: none -> 22.9 us  [exchanged(): return lax.all_to_all(parts, axis, split_axis=0, concat_axis=0, tiled=True)]
    unnamed x14 -> x5, local copies, waits for them, and re-layouts: 25.5 us -> 2.93 us
    all_to_all x5 -> x2, starting transfers between devices: 36 us -> 15.3 us  [exchanged(): return lax.all_to_all(parts, axis, split_axis=0, concat_axis=0, tiled=True)]
    split x5 -> x0, local copies, waits for them, and re-layouts: 15.1 us -> none  [in_one_piece(): jnp.split(lax.all_to_all(both, axis, split_axis=split_dim, concat_axis=co...]
    all_gather x0 -> x1, blocking collectives: none -> 13.2 us  [on_device(): router = lax.all_gather(rows, 'expert', axis=0, tiled=True)]
    convert_element_type x2 -> x0, other arithmetic: 6.37 us -> none  [the longest x1 6.36 us: on_device(): (w_up / jnp.expand_dims(scale_up, 1)).astype(jnp.bfloat16)]
  transfers between devices with their start and end apart: 5 -> 2, of which waited for: 3 -> 1; matrix products, arithmetic and copies ran while one was open for 17% -> 1% of each run, Pallas kernels for 0% -> 7%
where the time goes in v1:
time: 140 us; the launch traced here: 139 us
  waiting for transfers between devices  52 us (37%)
  blocking collectives  36.1 us (26%)
  Pallas kernels  30.4 us (22%)
  starting transfers between devices  15.3 us (11%)
  local copies, waits for them, and re-layouts  4.42 us (3%)
    all_to_all x2, waiting for transfers between devices, exchanged(): return lax.all_to_all(parts, axis, split_axis=0, concat_axis=0, tiled=True)  52 us
    all_to_all x1, blocking collectives, exchanged(): return lax.all_to_all(parts, axis, split_axis=0, concat_axis=0, tiled=True)  22.9 us
    all_to_all x2, starting transfers between devices, exchanged(): return lax.all_to_all(parts, axis, split_axis=0, concat_axis=0, tiled=True)  15.3 us
    all_gather x1, blocking collectives, on_device(): router = lax.all_gather(rows, 'expert', axis=0, tiled=True)  13.2 us
    pallas_call x1, Pallas kernels, turned(): pl.pallas_call(turned_kernel, grid=(width // LANES,), in_specs=[block, bl...  10.3 us
    pallas_call x1, Pallas kernels, scaled(): pl.pallas_call(functools.partial(scaled_kernel, own), grid=(size // part,...  9.28 us
    pallas_call x1, Pallas kernels, column_sums(): pl.pallas_call(functools.partial(sums_kernel, width // size), grid=(exper...  6.03 us
    pallas_call x1, Pallas kernels, placed(): pl.pallas_call(placed_kernel, grid=(own // part,), in_specs=[pl.BlockSpec...  4.84 us
  transfers between devices with their start and end apart: 2, of which 1 were waited for; matrix products, arithmetic and copies ran while one was open for 1% of the time, Pallas kernels for 7%

profile of v1, /device:TPU:8, one launch (start us, length us, event | category | flops | bytes accessed | tf_op | source)
XLA Modules:
  0.0 139.0 jit_solution(282885325974907779)
XLA Ops:
  0.6 6.0 %column_sums.1 = f32[32,2,8,128]{3,2,1,0:T(8,128)} custom-call(f32[8,64,1408]{2,1,0:T(8,128)} %gate_ref.3, f32[8,64,1408]{2,1,0:T(8,128)} %up_ref.3, f32[8,64]{1,0:T(8,128)} %bitcast.10, f32[1,64]{1,0:T(1,128)} %bitcast.11), custom_call_target="tpu_custom_call" | custom-call | flops 4000000 | bytes 6000000 | tf_op jit(solution)/shard_map/column_sums/pallas_call | solution.py:41
  6.7 22.9 %all_to_all.15 = f32[32,2,8,128]{3,2,1,0:T(8,128)S(1)} all-to-all(f32[32,2,8,128]{3,2,1,0:T(8,128)} %column_sums.1), channel_id=1, replica_groups=mesh['expert'=8,'shard'=32] {'shard'}, dimensions={0} | all-to-all | bytes 524288 | tf_op jit(solution)/shard_map/all_to_all | solution.py:126
  29.6 0.7 broadcast_in_dim.10
  30.3 5.6 %all-to-all-start.1 = ((f32[32,8,128]{2,1,0:T(8,128)}), f32[32,8,128]{2,1,0:T(8,128)S(1)}, u32[]{:S(2)}, u32[]{:S(2)}) async-start(f32[32,8,128]{2,1,0:T(8,128)} %broadcast_in_dim.10), calls=%async_computation.1 | async-start | bytes 262144 | tf_op jit(solution)/shard_map/all_to_all | solution.py:126
  35.9 10.3 %turned.1.turned_ref = f32[1408,8,128]{2,1,0:T(8,128)} custom-call(f32[8,64,1408]{2,1,0:T(8,128)} %gate_ref.3, f32[8,64,1408]{2,1,0:T(8,128)} %up_ref.3), custom_call_target="tpu_custom_call" | custom-call | flops 8000000 | bytes 12000000 | tf_op jit(solution)/shard_map/turned/pallas_call | solution.py:62
  46.1 0.0 all-to-all-done.1.scale_ref
  46.1 0.0 copy-start.1
  46.1 0.7 copy-done.1
  46.8 9.3 %scaled.1 = bf16[32,44,8,128]{3,2,1,0:T(8,128)(2,1)} custom-call(f32[1408,8,128]{2,1,0:T(8,128)} %turned.1.turned_ref, f32[32,8,128]{2,1,0:T(8,128)} %copy-done.1), custom_call_target="tpu_custom_call" | custom-call | flops 8000000 | bytes 9000000 | tf_op jit(solution)/shard_map/scaled/pallas_call | solution.py:87
  56.1 9.8 %all-to-all-start.2 = ((bf16[32,44,8,128]{3,2,1,0:T(8,128)(2,1)}), bf16[32,44,8,128]{3,2,1,0:T(8,128)(2,1)S(1)}, u32[]{:S(2)}, u32[]{:S(2)}) async-start(bf16[32,44,8,128]{3,2,1,0:T(8,128)(2,1)} %scaled.1), calls=%async_computation.2 | async-start | bytes 5767168 | tf_op jit(solution)/shard_map/all_to_all | solution.py:126
  65.9 0.1 reshape.17
  66.0 13.2 %all_gather.3 = bf16[64,2048]{1,0:T(8,128)(2,1)S(1)} all-gather(bf16[8,2048]{1,0:T(8,128)(2,1)S(1)} %reshape.17), channel_id=1, replica_groups=mesh['expert'=8,'shard'=32] {'expert'}, dimensions={0}, use_global_device_ids=true | all-gather | bytes 294912 | tf_op jit(solution)/shard_map/all_gather | solution.py:141
  79.2 0.7 fusion.1
  79.9 52.0 %all-to-all-done.2.arrived_ref = bf16[32,44,8,128]{3,2,1,0:T(8,128)(2,1)S(1)} async-done(((bf16[32,44,8,128]{3,2,1,0:T(8,128)(2,1)}), bf16[32,44,8,128]{3,2,1,0:T(8,128)(2,1)S(1)}, u32[]{:S(2)}, u32[]{:S(2)}) %all-to-all-start.2) | async-done | bytes 2883616 | tf_op jit(solution)/shard_map/all_to_all | solution.py:126
  131.9 0.0 copy-start
  131.9 1.6 %copy-done = bf16[32,44,8,128]{3,2,1,0:T(8,128)(2,1)} copy-done((bf16[32,44,8,128]{3,2,1,0:T(8,128)(2,1)}, bf16[32,44,8,128]{3,2,1,0:T(8,128)(2,1)S(1)}, u32[]{:S(2)}) %copy-start) | copy-done | bytes 2883608
  133.5 4.8 %placed.1 = (bf16[44,8,2048]{2,1,0:T(8,128)(2,1)}, bf16[44,8,2048]{2,1,0:T(8,128)(2,1)}) custom-call(bf16[32,44,8,128]{3,2,1,0:T(8,128)(2,1)} %copy-done), custom_call_target="tpu_custom_call" | custom-call | flops 4000000 | bytes 6000000 | tf_op jit(solution)/shard_map/placed/pallas_call | solution.py:114
  138.3 0.7 copy.11
  (4 shorter events, 0.1 us)
Async XLA Ops:
  30.3 15.9 %all-to-all-start.1 = ((f32[32,8,128]{2,1,0:T(8,128)}), f32[32,8,128]{2,1,0:T(8,128)S(1)}, u32[]{:S(2)}, u32[]{:S(2)}) async-start(f32[32,8,128]{2,1,0:T(8,128)} %broadcast_in_dim.10), calls=%async_computation.1 | async-start | bytes 262144 | tf_op jit(solution)/shard_map/all_to_all | solution.py:126
  46.1 0.7 copy-start.1
  56.1 75.8 %all-to-all-start.2 = ((bf16[32,44,8,128]{3,2,1,0:T(8,128)(2,1)}), bf16[32,44,8,128]{3,2,1,0:T(8,128)(2,1)S(1)}, u32[]{:S(2)}, u32[]{:S(2)}) async-start(bf16[32,44,8,128]{3,2,1,0:T(8,128)(2,1)} %scaled.1), calls=%async_computation.2 | async-start | bytes 5767168 | tf_op jit(solution)/shard_map/all_to_all | solution.py:126
  131.9 1.6 %copy-start = (bf16[32,44,8,128]{3,2,1,0:T(8,128)(2,1)}, bf16[32,44,8,128]{3,2,1,0:T(8,128)(2,1)S(1)}, u32[]{:S(2)}) copy-start(bf16[32,44,8,128]{3,2,1,0:T(8,128)(2,1)S(1)} %all-to-all-done.2.arrived_ref) | copy-start | bytes 8650756

commit v2 on v1

v2 whole, which is shorter than its diff:
```python
import jax
import jax.numpy as jnp
from jax import lax
from jax.experimental import pallas as pl
from jax.experimental.pallas import tpu as pltpu
from jax.sharding import PartitionSpec as P

D_MODEL = 2048
LANES = 128
HALF = LANES // 2
IN_HBM = pl.BlockSpec(memory_space=pltpu.HBM)
IN_VMEM = pl.BlockSpec(memory_space=pltpu.VMEM)


def in_hbm(x):
    return pltpu.with_memory_space_constraint(x, pltpu.HBM)


def in_vmem(x):
    return pltpu.with_memory_space_constraint(x, pltpu.VMEM)


def sums_kernel(
    gate, up, router, gain, out, gate_held, up_held,
    router_held, gain_held, sums, w_sems, small_sems, out_sem,
):
    experts = gate.shape[0]
    size = out.shape[0]
    own = gate.shape[2] // size
    small = [
        pltpu.make_async_copy(router, router_held, small_sems.at[0]),
        pltpu.make_async_copy(gain, gain_held, small_sems.at[1]),
    ]
    for copy in small:
        copy.start()
    pairs = [
        (
            pltpu.make_async_copy(gate.at[e], gate_held.at[e], w_sems.at[e, 0]),
            pltpu.make_async_copy(up.at[e], up_held.at[e], w_sems.at[e, 1]),
        )
        for e in range(experts)
    ]
    for pair in pairs:
        for copy in pair:
            copy.start()
    for copy in small:
        copy.wait()
    part = (router_held[...] * gain_held[...]).astype(jnp.bfloat16).astype(jnp.float32)
    part = jnp.concatenate([part, jnp.zeros_like(part)], axis=1)
    for d in range(size):
        sums[d, 1] = part
    gate_sums, up_sums = [], []
    for e in range(experts):
        pairs[e][0].wait()
        gate_sums.append(jnp.sum(jnp.abs(gate_held[e]), axis=0, keepdims=True))
        pairs[e][1].wait()
        up_sums.append(jnp.sum(jnp.abs(up_held[e]), axis=0, keepdims=True))
    gate_sums = jnp.concatenate(gate_sums, axis=0)
    up_sums = jnp.concatenate(up_sums, axis=0)
    spare = jnp.zeros((experts, HALF - own), jnp.float32)
    for d in range(size):
        columns = slice(d * own, (d + 1) * own)
        sums[d, 0] = jnp.concatenate(
            [gate_sums[:, columns], spare, up_sums[:, columns], spare], axis=1
        )
    copy = pltpu.make_async_copy(sums, out, out_sem)
    copy.start()
    copy.wait()


def column_sums(w_gate, w_up, router_weight, router_gain, size):
    experts = w_gate.shape[0]
    router, gain = router_weight.T, router_gain[None]
    shape = (size, 2, experts, LANES)
    return pl.pallas_call(
        sums_kernel,
        in_specs=[IN_HBM] * 4,
        out_specs=[IN_HBM, IN_VMEM, IN_VMEM],
        out_shape=[
            jax.ShapeDtypeStruct(shape, jnp.float32),
            pltpu.VMEM(w_gate.shape, jnp.float32),
            pltpu.VMEM(w_up.shape, jnp.float32),
        ],
        scratch_shapes=[
            pltpu.VMEM(router.shape, jnp.float32),
            pltpu.VMEM(gain.shape, jnp.float32),
            pltpu.VMEM(shape, jnp.float32),
            pltpu.SemaphoreType.DMA((experts, 2)),
            pltpu.SemaphoreType.DMA((2,)),
            pltpu.SemaphoreType.DMA,
        ],
        compiler_params=pltpu.CompilerParams(vmem_limit_bytes=8 << 20),
        cost_estimate=pl.CostEstimate(flops=4_000_000, bytes_accessed=6_000_000, transcendentals=0),
        name="column_sums",
    )(in_hbm(w_gate), in_hbm(w_up), in_hbm(router), in_hbm(gain))


def packed_kernel(gate, up, scales, out, held, sems):
    experts, _, width = gate.shape
    size = scales.shape[0]
    own = width // size
    gate_inverse = 1.0 / jnp.concatenate([scales[d, :, :own] for d in range(size)], axis=1)
    up_inverse = 1.0 / jnp.concatenate([scales[d, :, HALF : HALF + own] for d in range(size)], axis=1)
    copies = []
    for c in range(width // LANES):
        columns = slice(c * LANES, (c + 1) * LANES)
        turned = []
        for e in range(experts):
            both = jnp.concatenate(
                [
                    gate[e, :, columns] * gate_inverse[e : e + 1, columns],
                    up[e, :, columns] * up_inverse[e : e + 1, columns],
                ],
                axis=0,
            )
            turned.append(both.astype(jnp.bfloat16).T)
        held[columns] = jnp.swapaxes(jnp.stack(turned), 0, 1)
        rows = pl.ds(c * LANES, LANES)
        copies.append(pltpu.make_async_copy(held.at[rows], out.at[rows], sems.at[c]))
        copies[-1].start()
    for copy in copies:
        copy.wait()


def packed(w_gate, w_up, scales):
    experts, rows, width = w_gate.shape
    size = scales.shape[0]
    shape = (width, experts, 2 * rows)
    out = pl.pallas_call(
        packed_kernel,
        in_specs=[IN_VMEM] * 3,
        out_specs=IN_HBM,
        out_shape=pltpu.HBM(shape, jnp.bfloat16),
        scratch_shapes=[
            pltpu.VMEM(shape, jnp.bfloat16),
            pltpu.SemaphoreType.DMA((width // LANES,)),
        ],
        compiler_params=pltpu.CompilerParams(vmem_limit_bytes=12 << 20),
        cost_estimate=pl.CostEstimate(flops=8_000_000, bytes_accessed=9_000_000, transcendentals=0),
        name="packed",
    )(in_vmem(w_gate), in_vmem(w_up), in_vmem(scales))
    return out.reshape(size, width // size, experts, 2 * rows)


def placed_kernel(arrived, gate, up, gate_held, up_held, sems):
    size, total, _ = arrived.shape
    pieces = sems.shape[0]
    step = total // pieces
    copies = []
    for c in range(pieces):
        rows = slice(c * step, (c + 1) * step)
        for p in range(size // 2):
            first, second = arrived[2 * p, rows], arrived[2 * p + 1, rows]
            lanes = slice(p * LANES, (p + 1) * LANES)
            gate_held[rows, lanes] = jnp.concatenate([first[:, :HALF], second[:, :HALF]], axis=-1)
            up_held[rows, lanes] = jnp.concatenate([first[:, HALF:], second[:, HALF:]], axis=-1)
        part = pl.ds(c * step, step)
        for t, (held, out) in enumerate(((gate_held, gate), (up_held, up))):
            copies.append(pltpu.make_async_copy(held.at[part], out.at[part], sems.at[c, t]))
            copies[-1].start()
    for copy in copies:
        copy.wait()


def placed(arrived):
    size, own, experts, lanes = arrived.shape
    pieces = 11
    shape = (own * experts, size * HALF)
    out = jax.ShapeDtypeStruct(shape, jnp.bfloat16)
    results = pl.pallas_call(
        placed_kernel,
        in_specs=[IN_VMEM],
        out_specs=[IN_HBM] * 2,
        out_shape=[out, out],
        scratch_shapes=[
            pltpu.VMEM(shape, jnp.bfloat16),
            pltpu.VMEM(shape, jnp.bfloat16),
            pltpu.SemaphoreType.DMA((pieces, 2)),
        ],
        compiler_params=pltpu.CompilerParams(vmem_limit_bytes=12 << 20),
        cost_estimate=pl.CostEstimate(flops=4_000_000, bytes_accessed=6_000_000, transcendentals=0),
        name="placed",
    )(in_vmem(arrived.reshape(size, own * experts, lanes)))
    return [r.reshape(own, experts, size * HALF) for r in results]


def stored_kernel(held, out, sem):
    copy = pltpu.make_async_copy(held, out, sem)
    copy.start()
    copy.wait()


def stored(x):
    return pl.pallas_call(
        stored_kernel,
        in_specs=[IN_VMEM],
        out_specs=IN_HBM,
        out_shape=jax.ShapeDtypeStruct(x.shape, x.dtype),
        scratch_shapes=[pltpu.SemaphoreType.DMA],
        compiler_params=pltpu.CompilerParams(vmem_limit_bytes=1 << 20),
        cost_estimate=pl.CostEstimate(flops=1_000_000, bytes_accessed=500_000, transcendentals=0),
        name="stored",
    )(in_vmem(x))


def exchanged(parts, axis):
    return lax.all_to_all(parts, axis, split_axis=0, concat_axis=0, tiled=True)


def on_device(w_gate, w_up, router_weight, router_gain):
    size = lax.axis_size("shard")
    experts, _, width = w_gate.shape
    own = width // size
    sums, w_gate, w_up = column_sums(w_gate, w_up, router_weight, router_gain, size)
    arrived = exchanged(sums, "shard")
    scale = jnp.sum(arrived[:, 0], axis=0) / D_MODEL
    scales = exchanged(jnp.broadcast_to(scale[None], (size, *scale.shape)), "shard")
    serve = exchanged(packed(w_gate, w_up, scales), "shard")
    serve_gate, serve_up = placed(serve)
    rows = arrived[:, 1, :, :HALF].astype(jnp.bfloat16)
    rows = jnp.transpose(rows, (1, 0, 2)).reshape(experts, -1)
    router = lax.all_gather(rows, "expert", axis=0, tiled=True)
    return (
        jnp.transpose(serve_gate, (1, 2, 0)),
        jnp.transpose(serve_up, (1, 2, 0)),
        scale[:, :own],
        scale[:, HALF : HALF + own],
        stored(router).T,
    )


def solution(mesh):
    return jax.shard_map(
        on_device,
        mesh=mesh,
        in_specs=(
            P("expert", "shard", None),
            P("expert", "shard", None),
            P("shard", "expert"),
            P("shard"),
        ),
        out_specs=(
            P("expert", None, "shard"),
            P("expert", None, "shard"),
            P("expert", "shard"),
            P("expert", "shard"),
            P(),
        ),
        check_vma=False,
    )
```

time: 140 us -> 116 us (0.83)
  Pallas kernels: 30.4 us -> 7.93 us
  blocking collectives: 36.1 us -> 50.2 us
  starting transfers between devices: 15.3 us -> 5.55 us
  local copies, waits for them, and re-layouts: 4.42 us -> 0.83 us
    pallas_call x4, Pallas kernels: 30.4 us -> 7.93 us  [the longest x1 3.34 us: column_sums(): pl.pallas_call(sums_kernel, in_specs=[IN_HBM] * 4, out_specs=[IN_HBM, IN_...]
    all_to_all x1 -> x2, blocking collectives: 22.9 us -> 37 us  [exchanged(): return lax.all_to_all(parts, axis, split_axis=0, concat_axis=0, tiled=True)]
    all_to_all x2 -> x1, starting transfers between devices: 15.3 us -> 5.55 us  [exchanged(): return lax.all_to_all(parts, axis, split_axis=0, concat_axis=0, tiled=True)]
    unnamed x5 -> x0, local copies, waits for them, and re-layouts: 2.93 us -> none
    all_to_all x2 -> x1, waiting for transfers between devices: 52 us -> 50.8 us  [exchanged(): return lax.all_to_all(parts, axis, split_axis=0, concat_axis=0, tiled=True)]
  transfers between devices with their start and end apart: 2 -> 1, of which waited for: 1 -> 1; matrix products, arithmetic and copies ran while one was open for 1% -> 1% of each run, Pallas kernels for 7% -> 1%
where the time goes in v2:
time: 116 us
  waiting for transfers between devices  50.8 us (44%)
  blocking collectives  50.2 us (43%)
  Pallas kernels  7.93 us (7%)
  starting transfers between devices  5.55 us (5%)
    all_to_all x1, waiting for transfers between devices, exchanged(): return lax.all_to_all(parts, axis, split_axis=0, concat_axis=0, tiled=True)  50.8 us
    all_to_all x2, blocking collectives, exchanged(): return lax.all_to_all(parts, axis, split_axis=0, concat_axis=0, tiled=True)  37 us
    all_gather x1, blocking collectives, on_device(): router = lax.all_gather(rows, 'expert', axis=0, tiled=True)  13.2 us
    all_to_all x1, starting transfers between devices, exchanged(): return lax.all_to_all(parts, axis, split_axis=0, concat_axis=0, tiled=True)  5.55 us
    pallas_call x1, Pallas kernels, column_sums(): pl.pallas_call(sums_kernel, in_specs=[IN_HBM] * 4, out_specs=[IN_HBM, IN_...  3.34 us
  transfers between devices with their start and end apart: 1, of which 1 were waited for; matrix products, arithmetic and copies ran while one was open for 1% of the time, Pallas kernels for 1%

profile of v2, /device:TPU:8, one launch (start us, length us, event | category | flops | bytes accessed | tf_op | source)
XLA Modules:
  0.0 116.0 jit_solution(16838680357924388522)
XLA Ops:
  0.6 3.3 %column_sums.1 = (f32[32,2,8,128]{3,2,1,0:T(8,128)S(1)}, f32[8,64,1408]{2,1,0:T(8,128)S(1)}, f32[8,64,1408]{2,1,0:T(8,128)S(1)}) custom-call(f32[8,64,1408]{2,1,0:T(8,128)} %gate.1, f32[8,64,1408]{2,1,0:T(8,128)} %up.1, f32[8,64]{1,0:T(8,128)} %bitcast.18, f32[1,64]{1,0:T(1,128)} %bitcast.19), custom_call_target="tpu_custom_call" | custom-call | flops 4000000 | bytes 6000000 | tf_op jit(solution)/shard_map/column_sums/pallas_call | solution.py:75
  4.0 22.7 %all_to_all.15 = f32[32,2,8,128]{3,2,1,0:T(8,128)S(1)} all-to-all(f32[32,2,8,128]{3,2,1,0:T(8,128)S(1)} %get-tuple-element.12), channel_id=1, replica_groups=mesh['expert'=8,'shard'=32] {'shard'}, dimensions={0} | all-to-all | bytes 524288 | tf_op jit(solution)/shard_map/all_to_all | solution.py:207
  26.7 14.3 %all_to_all.16.scales = f32[32,8,128]{2,1,0:T(8,128)S(1)} all-to-all(f32[32,8,128]{2,1,0:T(8,128)S(1)} %broadcast_in_dim.10), channel_id=1, replica_groups=mesh['expert'=8,'shard'=32] {'shard'}, dimensions={0} | all-to-all | bytes 262144 | tf_op jit(solution)/shard_map/all_to_all | solution.py:207
  41.1 2.0 %packed.1 = bf16[1408,8,128]{2,1,0:T(8,128)(2,1)} custom-call(f32[8,64,1408]{2,1,0:T(8,128)S(1)} %get-tuple-element.10.gate, f32[8,64,1408]{2,1,0:T(8,128)S(1)} %get-tuple-element.11.up, f32[32,8,128]{2,1,0:T(8,128)S(1)} %all_to_all.16.scales), custom_call_target="tpu_custom_call" | custom-call | flops 8000000 | bytes 9000000 | tf_op jit(solution)/shard_map/packed/pallas_call | solution.py:129
  43.1 5.6 %all-to-all-start.2 = ((bf16[32,44,8,128]{3,2,1,0:T(8,128)(2,1)}), bf16[32,44,8,128]{3,2,1,0:T(8,128)(2,1)S(1)}, u32[]{:S(2)}, u32[]{:S(2)}) async-start(bf16[32,44,8,128]{3,2,1,0:T(8,128)(2,1)} %bitcast.16), calls=%async_computation.2 | async-start | bytes 5767168 | tf_op jit(solution)/shard_map/all_to_all | solution.py:207
  48.7 0.1 reshape.33
  48.8 13.2 %all_gather.3.held = bf16[64,2048]{1,0:T(8,128)(2,1)S(1)} all-gather(bf16[8,2048]{1,0:T(8,128)(2,1)S(1)} %reshape.33), channel_id=1, replica_groups=mesh['expert'=8,'shard'=32] {'expert'}, dimensions={0}, use_global_device_ids=true | all-gather | bytes 294912 | tf_op jit(solution)/shard_map/all_gather | solution.py:222
  62.0 0.7 stored.1
  62.7 0.7 fusion.1
  63.4 50.8 %all-to-all-done.2 = bf16[32,44,8,128]{3,2,1,0:T(8,128)(2,1)S(1)} async-done(((bf16[32,44,8,128]{3,2,1,0:T(8,128)(2,1)}), bf16[32,44,8,128]{3,2,1,0:T(8,128)(2,1)S(1)}, u32[]{:S(2)}, u32[]{:S(2)}) %all-to-all-start.2) | async-done | bytes 2883616 | tf_op jit(solution)/shard_map/all_to_all | solution.py:207
  114.1 1.9 %placed.1 = (bf16[352,2048]{1,0:T(8,128)(2,1)}, bf16[352,2048]{1,0:T(8,128)(2,1)}) custom-call(bf16[32,352,128]{2,1,0:T(8,128)(2,1)S(1)} %bitcast.15), custom_call_target="tpu_custom_call" | custom-call | flops 4000000 | bytes 6000000 | tf_op jit(solution)/shard_map/placed/pallas_call | solution.py:170
  (5 shorter events, 0.1 us)
Async XLA Ops:
  43.1 71.1 %all-to-all-start.2 = ((bf16[32,44,8,128]{3,2,1,0:T(8,128)(2,1)}), bf16[32,44,8,128]{3,2,1,0:T(8,128)(2,1)S(1)}, u32[]{:S(2)}, u32[]{:S(2)}) async-start(bf16[32,44,8,128]{3,2,1,0:T(8,128)(2,1)} %bitcast.16), calls=%async_computation.2 | async-start | bytes 5767168 | tf_op jit(solution)/shard_map/all_to_all | solution.py:207

commit v3 on v2

v3 whole, which is shorter than its diff:
```python
import functools

import jax
import jax.numpy as jnp
from jax import lax
from jax.experimental import pallas as pl
from jax.experimental.pallas import tpu as pltpu
from jax.sharding import PartitionSpec as P


D_MODEL = 2048
LANES = 128
HALF = LANES // 2
Z, Y = 8, 4
ALONG_Y = [[z * Y + y for y in range(Y)] for z in range(Z)]
ALONG_Z = [[z * Y + y for z in range(Z)] for y in range(Y)]
SHIFTS = (0, 1, 7, 4, 3, 5, 2, 6)
RAW = 8
PIECE = 80
HEAD = 6 * LANES
IN_HBM = pl.BlockSpec(memory_space=pltpu.HBM)
IN_VMEM = pl.BlockSpec(memory_space=pltpu.VMEM)


def in_hbm(x):
    return pltpu.with_memory_space_constraint(x, pltpu.HBM)


def in_vmem(x):
    return pltpu.with_memory_space_constraint(x, pltpu.VMEM)


def opened_kernel(gate, up, router, gain, *refs):
    out, gate_head, up_head, *blocks = refs[: 3 + Z]
    (
        gate_tail, up_tail, router_held, gain_held, sums, held, w_sems, small_sems, sums_sem, block_sems,
    ) = refs[3 + Z :]
    experts, _, width = gate.shape
    own = width // (Y * Z)
    loads = [
        [
            (
                pltpu.make_async_copy(w.at[e, :, pl.ds(0, HEAD)], head.at[e], w_sems.at[e, t, 0]),
                pltpu.make_async_copy(
                    w.at[e, :, pl.ds(HEAD, width - HEAD)], tail.at[e], w_sems.at[e, t, 1]
                ),
            )
            for t, (w, head, tail) in enumerate(((gate, gate_head, gate_tail), (up, up_head, up_tail)))
        ]
        for e in range(experts)
    ]
    small = [
        pltpu.make_async_copy(router, router_held, small_sems.at[0]),
        pltpu.make_async_copy(gain, gain_held, small_sems.at[1]),
    ]
    for pairs in loads:
        for pair in pairs:
            for copy in pair:
                copy.start()
    for copy in small:
        copy.start()
    rows = ([], [])
    for e in range(experts):
        for t, (head, tail) in enumerate(((gate_head, gate_tail), (up_head, up_tail))):
            totals = []
            for part, copy in zip((head, tail), loads[e][t]):
                copy.wait()
                totals.append(jnp.sum(jnp.abs(part[e]), axis=0, keepdims=True))
            rows[t].append(jnp.concatenate(totals, axis=1))
    gate_sums, up_sums = (jnp.concatenate(r, axis=0) for r in rows)
    spare = jnp.zeros((experts, HALF - own), jnp.float32)
    for d in range(Y * Z):
        mine = slice(d * own, (d + 1) * own)
        sums[d % Y, d // Y] = jnp.concatenate([gate_sums[:, mine], spare, up_sums[:, mine], spare], axis=1)
    copies = [pltpu.make_async_copy(sums, out, sums_sem)]
    copies[0].start()
    for copy in small:
        copy.wait()
    part = (router_held[...] * gain_held[...]).astype(jnp.bfloat16).astype(jnp.float32)
    part = jnp.concatenate([part, jnp.zeros_like(part)], axis=1)
    for z in range(Z):
        held[z, Y * RAW] = part
    for c in range(width // LANES):
        if c * LANES < HEAD:
            sources, first = (gate_head, up_head), c * LANES
        else:
            sources, first = (gate_tail, up_tail), c * LANES - HEAD
        columns = slice(first, first + LANES)
        turned = [jnp.concatenate([w[e, :, columns] for w in sources], axis=0).T for e in range(experts)]
        for d in range(Y * Z):
            low = max(d * own, c * LANES)
            high = min(d * own + RAW, (c + 1) * LANES)
            if low < high:
                part = jnp.stack([t[low - c * LANES : high - c * LANES] for t in turned])
                place = slice(d % Y * RAW + low - d * own, d % Y * RAW + high - d * own)
                held[d // Y, place] = jnp.swapaxes(part, 0, 1)
    z = lax.axis_index("shard") // Y
    for k, shift in enumerate(SHIFTS):
        copies.append(pltpu.make_async_copy(held.at[lax.rem(z + shift, Z)], blocks[k], block_sems.at[k]))
        copies[-1].start()
    for copy in copies:
        copy.wait()


def opened(w_gate, w_up, router_weight, router_gain):
    experts, rows, width = w_gate.shape
    router, gain = router_weight.T, router_gain[None]
    shape = (Y, Z, experts, LANES)
    block = (Y * RAW + 1, experts, LANES)
    head = pltpu.VMEM((experts, rows, HEAD), jnp.float32)
    tail = pltpu.VMEM((experts, rows, width - HEAD), jnp.float32)
    out, gate_head, up_head, *blocks = pl.pallas_call(
        opened_kernel,
        in_specs=[IN_HBM] * 4,
        out_specs=[IN_HBM, IN_VMEM, IN_VMEM] + [IN_HBM] * Z,
        out_shape=[pltpu.HBM(shape, jnp.float32), head, head] + [pltpu.HBM(block, jnp.float32)] * Z,
        scratch_shapes=[
            tail,
            tail,
            pltpu.VMEM(router.shape, jnp.float32),
            pltpu.VMEM(gain.shape, jnp.float32),
            pltpu.VMEM(shape, jnp.float32),
            pltpu.VMEM((Z, *block), jnp.float32),
            pltpu.SemaphoreType.DMA((experts, 2, 2)),
            pltpu.SemaphoreType.DMA((2,)),
            pltpu.SemaphoreType.DMA,
            pltpu.SemaphoreType.DMA((Z,)),
        ],
        compiler_params=pltpu.CompilerParams(vmem_limit_bytes=10 << 20),
        cost_estimate=pl.CostEstimate(flops=8_000_000, bytes_accessed=8_000_000, transcendentals=0),
        name="opened",
    )(in_hbm(w_gate), in_hbm(w_up), in_hbm(router), in_hbm(gain))
    return out, (gate_head, up_head), blocks


def regrouped_kernel(*refs):
    blocks, outs, pieces = refs[:Z], refs[Z : Z + Y], refs[Z + Y]
    held, in_sems, out_sems, piece_sem = refs[Z + Y + 1 :]
    y = lax.rem(lax.axis_index("shard"), Y)
    copies = [pltpu.make_async_copy(blocks[k], held.at[k], in_sems.at[k]) for k in range(Z)]
    for copy in copies:
        copy.start()
    for copy in copies:
        copy.wait()
    copies = [pltpu.make_async_copy(held.at[:, Y * RAW], pieces, piece_sem)] + [
        pltpu.make_async_copy(
            held.at[:, pl.ds(lax.rem(y + t, Y) * RAW, RAW)], outs[t], out_sems.at[t]
        )
        for t in range(Y)
    ]
    for copy in copies:
        copy.start()
    for copy in copies:
        copy.wait()


def regrouped(blocks):
    rest = blocks[0].shape[1:]
    return pl.pallas_call(
        regrouped_kernel,
        in_specs=[IN_HBM] * Z,
        out_specs=[IN_HBM] * (Y + 1),
        out_shape=[pltpu.HBM((Z, RAW, *rest), jnp.float32)] * Y + [pltpu.HBM((Z, *rest), jnp.float32)],
        scratch_shapes=[
            pltpu.VMEM((Z, *blocks[0].shape), jnp.float32),
            pltpu.SemaphoreType.DMA((Z,)),
            pltpu.SemaphoreType.DMA((Y,)),
            pltpu.SemaphoreType.DMA,
        ],
        compiler_params=pltpu.CompilerParams(vmem_limit_bytes=3 << 20),
        cost_estimate=pl.CostEstimate(flops=8_000_000, bytes_accessed=2_000_000, transcendentals=0),
        name="regrouped",
    )(*[in_hbm(b) for b in blocks])


def in_source_order(blocks, held, sems):
    me = lax.axis_index("shard")
    z, y = me // Y, lax.rem(me, Y)
    copies = []
    for t in range(Y):
        for k, shift in enumerate(SHIFTS):
            source = lax.rem(z + Z - shift, Z) * Y + lax.rem(y + Y - t, Y)
            copies.append(pltpu.make_async_copy(blocks[t].at[k], held.at[source], sems.at[t, k]))
    return copies


def rows_kernel(*refs):
    blocks, router, (held, sems) = refs[:Y], refs[Y], refs[Y + 1 :]
    copies = in_source_order(blocks, held, sems)
    for copy in copies:
        copy.start()
    for copy in copies:
        copy.wait()
    for p in range(Y * Z // 2):
        both = jnp.concatenate([held[2 * p][:, :HALF], held[2 * p + 1][:, :HALF]], axis=1)
        router[:, p * LANES : (p + 1) * LANES] = both.astype(jnp.bfloat16)


def router_rows(pieces):
    experts = pieces[0].shape[1]
    return pl.pallas_call(
        rows_kernel,
        in_specs=[IN_HBM] * Y,
        out_specs=IN_VMEM,
        out_shape=pltpu.VMEM((experts, Y * Z * HALF), jnp.bfloat16),
        scratch_shapes=[
            pltpu.VMEM((Y * Z, *pieces[0].shape[1:]), jnp.float32),
            pltpu.SemaphoreType.DMA((Y, Z)),
        ],
        compiler_params=pltpu.CompilerParams(vmem_limit_bytes=1 << 20),
        cost_estimate=pl.CostEstimate(flops=1_000_000, bytes_accessed=300_000, transcendentals=0),
        name="router_rows",
    )(*[in_hbm(b) for b in pieces])


def finished_kernel(*refs):
    blocks, scale, (gate, up), (held, sems) = refs[:Y], refs[Y], refs[Y + 1 : Y + 3], refs[Y + 3 :]
    copies = in_source_order(blocks, held, sems)
    for copy in copies:
        copy.start()
    inverse = 1.0 / scale[...]
    rows = inverse.shape[0]
    for copy in copies:
        copy.wait()
    for p in range(Y * Z // 2):
        lanes = slice(p * LANES, (p + 1) * LANES)
        for j in range(RAW):
            first, second = held[2 * p, j], held[2 * p + 1, j]
            place = slice(j * rows, (j + 1) * rows)
            for out, low in ((gate, 0), (up, HALF)):
                factor = jnp.broadcast_to(inverse[:, low + j : low + j + 1], (rows, LANES))
                both = jnp.concatenate([first[:, low : low + HALF], second[:, low : low + HALF]], axis=1)
                out[place, lanes] = (both * factor).astype(jnp.bfloat16)


def finished(blocks, scale):
    experts = scale.shape[0]
    out = pltpu.VMEM((RAW * experts, Y * Z * HALF), jnp.bfloat16)
    return pl.pallas_call(
        finished_kernel,
        in_specs=[IN_HBM] * Y + [IN_VMEM],
        out_specs=[IN_VMEM] * 2,
        out_shape=[out, out],
        scratch_shapes=[
            pltpu.VMEM((Y * Z, *blocks[0].shape[1:]), jnp.float32),
            pltpu.SemaphoreType.DMA((Y, Z)),
        ],
        compiler_params=pltpu.CompilerParams(vmem_limit_bytes=6 << 20),
        cost_estimate=pl.CostEstimate(flops=8_000_000, bytes_accessed=3_000_000, transcendentals=0),
        name="finished",
    )(*[in_hbm(b) for b in blocks], in_vmem(scale))


def packed_kernel(gate, up, gate_head, up_head, scales, out, tails, held, tail_sems, sems):
    experts, _, width = gate.shape
    size = Y * Z
    loads = [
        [
            pltpu.make_async_copy(w.at[:, :, pl.ds(low, LANES)], tails.at[c, t], tail_sems.at[c, t])
            for t, w in enumerate((gate, up))
        ]
        for c, low in enumerate(range(HEAD, width, LANES))
    ]
    for pair in loads:
        for copy in pair:
            copy.start()
    own = width // size
    tiles = [scales[d % Y, d // Y] for d in range(size)]
    gate_inverse = 1.0 / jnp.concatenate([t[:, :own] for t in tiles], axis=1)
    up_inverse = 1.0 / jnp.concatenate([t[:, HALF : HALF + own] for t in tiles], axis=1)
    copies = []
    for c in range(width // LANES):
        columns = slice(c * LANES, (c + 1) * LANES)
        tail = c - HEAD // LANES
        if tail >= 0:
            for copy in loads[tail]:
                copy.wait()
        turned = []
        for e in range(experts):
            if tail < 0:
                parts = gate_head[e, :, columns], up_head[e, :, columns]
            else:
                parts = tails[tail, 0, e], tails[tail, 1, e]
            both = jnp.concatenate(
                [
                    parts[0] * gate_inverse[e : e + 1, columns],
                    parts[1] * up_inverse[e : e + 1, columns],
                ],
                axis=0,
            )
            turned.append(both.astype(jnp.bfloat16).T)
        held[columns] = jnp.swapaxes(jnp.stack(turned), 0, 1)
        while len(copies) < size and (len(copies) + 1) * own <= (c + 1) * LANES:
            d = len(copies)
            rows = pl.ds(d * own + RAW, own - RAW)
            copies.append(pltpu.make_async_copy(held.at[rows], out.at[d], sems.at[d]))
            copies[-1].start()
    for copy in copies:
        copy.wait()


def packed(w_gate, w_up, gate_head, up_head, scales):
    experts, rows, width = w_gate.shape
    size = Y * Z
    return pl.pallas_call(
        packed_kernel,
        in_specs=[IN_HBM] * 2 + [IN_VMEM] * 3,
        out_specs=IN_HBM,
        out_shape=pltpu.HBM((size, width // size - RAW, experts, 2 * rows), jnp.bfloat16),
        scratch_shapes=[
            pltpu.VMEM(((width - HEAD) // LANES, 2, experts, rows, LANES), jnp.float32),
            pltpu.VMEM((width, experts, 2 * rows), jnp.bfloat16),
            pltpu.SemaphoreType.DMA(((width - HEAD) // LANES, 2)),
            pltpu.SemaphoreType.DMA((size,)),
        ],
        compiler_params=pltpu.CompilerParams(vmem_limit_bytes=12 << 20),
        cost_estimate=pl.CostEstimate(flops=8_000_000, bytes_accessed=9_000_000, transcendentals=0),
        name="packed",
    )(in_hbm(w_gate), in_hbm(w_up), in_vmem(gate_head), in_vmem(up_head), in_vmem(scales))


def placed_kernel(arrived, raw_gate, raw_up, gate, up, gate_held, up_held, raw_sems, sems):
    size, total, _ = arrived.shape
    raw = raw_gate.shape[0]
    copies = []
    for t, (part, out) in enumerate(((raw_gate, gate), (raw_up, up))):
        copies.append(pltpu.make_async_copy(part, out.at[pl.ds(0, raw)], raw_sems.at[t]))
        copies[-1].start()
    for c, low in enumerate(range(0, total, PIECE)):
        high = min(low + PIECE, total)
        rows = slice(low, high)
        for p in range(size // 2):
            first, second = arrived[2 * p, rows], arrived[2 * p + 1, rows]
            lanes = slice(p * LANES, (p + 1) * LANES)
            gate_held[rows, lanes] = jnp.concatenate([first[:, :HALF], second[:, :HALF]], axis=-1)
            up_held[rows, lanes] = jnp.concatenate([first[:, HALF:], second[:, HALF:]], axis=-1)
        for t, (held, out) in enumerate(((gate_held, gate), (up_held, up))):
            copies.append(
                pltpu.make_async_copy(
                    held.at[pl.ds(low, high - low)],
                    out.at[pl.ds(raw + low, high - low)],
                    sems.at[c, t],
                )
            )
            copies[-1].start()
    for copy in copies:
        copy.wait()


def placed(arrived, raw_gate, raw_up):
    size, rest, experts, lanes = arrived.shape
    held = (rest * experts, size * HALF)
    shape = ((rest + RAW) * experts, size * HALF)
    out = jax.ShapeDtypeStruct(shape, jnp.bfloat16)
    results = pl.pallas_call(
        placed_kernel,
        in_specs=[IN_VMEM] * 3,
        out_specs=[IN_HBM] * 2,
        out_shape=[out, out],
        scratch_shapes=[
            pltpu.VMEM(held, jnp.bfloat16),
            pltpu.VMEM(held, jnp.bfloat16),
            pltpu.SemaphoreType.DMA((2,)),
            pltpu.SemaphoreType.DMA((pl.cdiv(held[0], PIECE), 2)),
        ],
        compiler_params=pltpu.CompilerParams(vmem_limit_bytes=12 << 20),
        cost_estimate=pl.CostEstimate(flops=4_000_000, bytes_accessed=6_000_000, transcendentals=0),
        name="placed",
    )(in_vmem(arrived.reshape(size, rest * experts, lanes)), in_vmem(raw_gate), in_vmem(raw_up))
    return [r.reshape(rest + RAW, experts, size * HALF) for r in results]


def stored_kernel(held, out, sem):
    copy = pltpu.make_async_copy(held, out, sem)
    copy.start()
    copy.wait()


def stored(x):
    return pl.pallas_call(
        stored_kernel,
        in_specs=[IN_VMEM],
        out_specs=IN_HBM,
        out_shape=jax.ShapeDtypeStruct(x.shape, x.dtype),
        scratch_shapes=[pltpu.SemaphoreType.DMA],
        compiler_params=pltpu.CompilerParams(vmem_limit_bytes=1 << 20),
        cost_estimate=pl.CostEstimate(flops=1_000_000, bytes_accessed=500_000, transcendentals=0),
        name="stored",
    )(in_vmem(x))


def summed_kernel(share, arrived, out, *refs):
    *mine, held, sems = refs
    held[...] = jnp.sum(arrived[...], axis=0) * share
    copies = [pltpu.make_async_copy(held, out.at[i], sems.at[i]) for i in range(out.shape[0])]
    for copy in copies:
        copy.start()
    for ref in mine:
        ref[...] = held[lax.axis_index("shard") // Y]
    for copy in copies:
        copy.wait()


def summed(arrived, count, share, mine=False):
    shape = arrived.shape[1:]
    return pl.pallas_call(
        functools.partial(summed_kernel, share),
        in_specs=[IN_VMEM],
        out_specs=[IN_HBM, IN_VMEM][: 1 + mine],
        out_shape=[
            pltpu.HBM((count, *shape), jnp.float32),
            pltpu.VMEM(shape[1:], jnp.float32),
        ][: 1 + mine],
        scratch_shapes=[pltpu.VMEM(shape, jnp.float32), pltpu.SemaphoreType.DMA((count,))],
        compiler_params=pltpu.CompilerParams(vmem_limit_bytes=1 << 20),
        cost_estimate=pl.CostEstimate(flops=1_000_000, bytes_accessed=500_000, transcendentals=0),
        name="summed",
    )(in_vmem(arrived))


def exchanged(parts, groups=None):
    return lax.all_to_all(
        parts, "shard", split_axis=0, concat_axis=0, tiled=True, axis_index_groups=groups
    )


def shifted(x, z_shift, y_shift):
    pairs = [
        (z * Y + y, (z + z_shift) % Z * Y + (y + y_shift) % Y) for z in range(Z) for y in range(Y)
    ]
    return lax.ppermute(x, "shard", pairs)


def on_device(w_gate, w_up, router_weight, router_gain):
    own = w_gate.shape[2] // (Y * Z)
    sums, heads, blocks = opened(w_gate, w_up, router_weight, router_gain)
    sums = exchanged(sums, ALONG_Y)
    (sums,) = summed(sums, Z, 1.0)
    sums = exchanged(sums, ALONG_Z)
    moved = [blocks[0]]
    for k, shift in enumerate(SHIFTS):
        if k:
            moved.append(shifted(blocks[k], shift, 0))
    scales, scale = summed(sums, Y, 1.0 / D_MODEL, mine=True)
    scales = exchanged(scales, ALONG_Y)
    serve = packed(w_gate, w_up, *heads, scales)
    serve = exchanged(serve)
    *moved, pieces = regrouped(moved)
    pieces = [pieces]
    for t in range(1, Y):
        pieces.append(shifted(pieces[0], 0, t))
    for t in range(1, Y):
        moved[t] = shifted(moved[t], 0, t)
    rows = router_rows(pieces)
    router = lax.all_gather(rows, "expert", axis=0, tiled=True)
    router = stored(router)
    raw_gate, raw_up = finished(moved, scale)
    serve_gate, serve_up = placed(serve, raw_gate, raw_up)
    return (
        jnp.transpose(serve_gate, (1, 2, 0)),
        jnp.transpose(serve_up, (1, 2, 0)),
        scale[:, :own],
        scale[:, HALF : HALF + own],
        router.T,
    )


def solution(mesh):
    return jax.shard_map(
        on_device,
        mesh=mesh,
        in_specs=(
            P("expert", "shard", None),
            P("expert", "shard", None),
            P("shard", "expert"),
            P("shard"),
        ),
        out_specs=(
            P("expert", None, "shard"),
            P("expert", None, "shard"),
            P("expert", "shard"),
            P("expert", "shard"),
            P(),
        ),
        check_vma=False,
    )
```

time: 116 us -> 171 us (1.47)
  the two profiles are of different devices: /device:TPU:8 before, /device:TPU:65 now
where the time goes in v3:
time: 171 us
  waiting for transfers between devices  68 us (40%)
  blocking collectives  51.6 us (30%)
  starting transfers between devices  28.3 us (17%)
  Pallas kernels  18.8 us (11%)
  local copies, waits for them, and re-layouts  2.8 us (2%)
    ppermute x13, waiting for transfers between devices, shifted(): return lax.ppermute(x, 'shard', pairs)  68 us
    all_to_all x3, blocking collectives, exchanged(): lax.all_to_all(parts, 'shard', split_axis=0, concat_axis=0, tiled=True, a...  31.3 us
    ppermute x13, starting transfers between devices, shifted(): return lax.ppermute(x, 'shard', pairs)  21.5 us
    all_gather x1, blocking collectives, on_device(): router = lax.all_gather(rows, 'expert', axis=0, tiled=True)  20.3 us
    all_to_all x1, starting transfers between devices, exchanged(): lax.all_to_all(parts, 'shard', split_axis=0, concat_axis=0, tiled=True, a...  6.76 us
    pallas_call x1, Pallas kernels, opened(): pl.pallas_call(opened_kernel, in_specs=[IN_HBM] * 4, out_specs=[IN_HBM, I...  5.77 us
    pallas_call x1, Pallas kernels, packed(): pl.pallas_call(packed_kernel, in_specs=[IN_HBM] * 2 + [IN_VMEM] * 3, out_...  3.72 us
  transfers between devices with their start and end apart: 14, of which 9 were waited for; matrix products, arithmetic and copies ran while one was open for 0% of the time, Pallas kernels for 4%

profile of v3, /device:TPU:65, one launch (start us, length us, event | category | flops | bytes accessed | tf_op | source)
XLA Modules:
  0.0 170.6 jit_solution(17080694763373919040)
XLA Ops:
  0.6 5.8 %opened.1 = (f32[4,8,8,128]{3,2,1,0:T(8,128)}, f32[8,64,768]{2,1,0:T(8,128)S(1)}, f32[8,64,768]{2,1,0:T(8,128)S(1)}, f32[33,8,128]{2,1,0:T(8,128)}, f32[33,8,128...) custom-call(f32[8,64,1408]{2,1,0:T(8,128)} %gate.3, ...), custom_call_target="tpu_custom_call" | custom-call | flops 8000000 | bytes 8000000 | tf_op jit(solution)/shard_map/opened/pallas_call | solution.py:112
  6.4 9.0 %all_to_all.20.arrived = f32[4,8,8,128]{3,2,1,0:T(8,128)S(1)} all-to-all(f32[4,8,8,128]{3,2,1,0:T(8,128)} %get-tuple-element.29), channel_id=1, replica_groups={{0,1,2,3},{4,5,6,7},{8,9,10,11},{12,13,14,15},{16,17,18,19},{20,21,22,2..., dimensions={0} | all-to-all | bytes 262144 | tf_op jit(solution)/shard_map/all_to_all | solution.py:422
  16.2 14.2 %all_to_all.21.arrived = f32[8,8,8,128]{3,2,1,0:T(8,128)S(1)} all-to-all(f32[8,8,8,128]{3,2,1,0:T(8,128)} %summed.2), channel_id=1, replica_groups={{0,4,8,12,16,20,24,28},{1,5,9,13,17,21,25,29},{2,6,10,14,18,22,26,30},{..., dimensions={0} | all-to-all | bytes 524288 | tf_op jit(solution)/shard_map/all_to_all | solution.py:422
  31.1 8.1 %all_to_all.22.scales = f32[4,8,8,128]{3,2,1,0:T(8,128)S(1)} all-to-all(f32[4,8,8,128]{3,2,1,0:T(8,128)} %get-tuple-element.30), channel_id=1, replica_groups={{0,1,2,3},{4,5,6,7},{8,9,10,11},{12,13,14,15},{16,17,18,19},{20,21,22,2..., dimensions={0} | all-to-all | bytes 262144 | tf_op jit(solution)/shard_map/all_to_all | solution.py:422
  39.2 3.7 %packed.1 = bf16[32,36,8,128]{3,2,1,0:T(8,128)(2,1)} custom-call(f32[8,64,1408]{2,1,0:T(8,128)} %gate.3, f32[8,64,1408]{2,1,0:T(8,128)} %up.3, f32[8,64,768]{2,1,0:T(8,128)S(1)} %get-tuple-element.27.gate_head, f32[8,64,768]{2,1,0:T(8,128)S(1)} %get-tuple-element.28.up_head, f32[4,8,8,128]{3,2,1,0:T(8,128)S(1)} %all_to_all.22.scales), custom_call_target="tpu_custom_call" | custom-call | flops 8000000 | bytes 9000000 | tf_op jit(solution)/shard_map/packed/pallas_call | solution.py:305
  43.0 6.8 %all-to-all-start.3 = ((bf16[32,36,8,128]{3,2,1,0:T(8,128)(2,1)}), bf16[32,36,8,128]{3,2,1,0:T(8,128)(2,1)S(1)}, u32[]{:S(2)}, u32[]{:S(2)}) async-start(bf16[32,36,8,128]{3,2,1,0:T(8,128)(2,1)} %packed.1), calls=%async_computation.3 | async-start | bytes 4718592 | tf_op jit(solution)/shard_map/all_to_all | solution.py:422
  49.8 1.3 collective-permute-start
  51.3 3.4 %collective-permute-start.2 = (f32[33,8,128]{2,1,0:T(8,128)S(1)}, f32[33,8,128]{2,1,0:T(8,128)S(1)}, u32[]{:S(2)}, u32[]{:S(2)}) collective-permute-start(f32[33,8,128]{2,1,0:T(8,128)S(1)} %copy-done.17), channel_id=1, source_target_pairs={{0,16},{1,17},{2,18},{3,19},{4,20},{5,21},{6,22},{7,23},{8,24},{9,... | collective-permute-start | bytes 405512 | tf_op jit(solution)/shard_map/ppermute | solution.py:431
  55.8 3.4 %collective-permute-start.4 = (f32[33,8,128]{2,1,0:T(8,128)S(1)}, f32[33,8,128]{2,1,0:T(8,128)S(1)}, u32[]{:S(2)}, u32[]{:S(2)}) collective-permute-start(f32[33,8,128]{2,1,0:T(8,128)S(1)} %copy-done.15), channel_id=1, source_target_pairs={{0,20},{1,21},{2,22},{3,23},{4,24},{5,25},{6,26},{7,27},{8,28},{9,... | collective-permute-start | bytes 405512 | tf_op jit(solution)/shard_map/ppermute | solution.py:431
  59.2 47.1 %collective-permute-done.refs_1_ = f32[33,8,128]{2,1,0:T(8,128)S(1)} collective-permute-done((f32[33,8,128]{2,1,0:T(8,128)S(1)}, f32[33,8,128]{2,1,0:T(8,128)S(1)}, u32[]{:S(2)}, u32[]{:S(2)}) %collective-permute-start) | collective-permute-done | bytes 135200 | tf_op jit(solution)/shard_map/ppermute | solution.py:431
  106.3 2.4 %collective-permute-start.6 = (f32[33,8,128]{2,1,0:T(8,128)S(1)}, f32[33,8,128]{2,1,0:T(8,128)S(1)}, u32[]{:S(2)}, u32[]{:S(2)}) collective-permute-start(f32[33,8,128]{2,1,0:T(8,128)S(1)} %copy-done.13), channel_id=1, source_target_pairs={{0,24},{1,25},{2,26},{3,27},{4,28},{5,29},{6,30},{7,31},{8,0},{9,1... | collective-permute-start | bytes 405512 | tf_op jit(solution)/shard_map/ppermute | solution.py:431
  108.7 1.6 collective-permute-done.2.refs_3_
  110.3 2.9 %collective-permute-done.3.refs_4_ = f32[33,8,128]{2,1,0:T(8,128)S(1)} collective-permute-done((f32[33,8,128]{2,1,0:T(8,128)S(1)}, f32[33,8,128]{2,1,0:T(8,128)S(1)}, u32[]{:S(2)}, u32[]{:S(2)}) %collective-permute-start.3) | collective-permute-done | bytes 135200 | tf_op jit(solution)/shard_map/ppermute | solution.py:431
  113.3 2.3 %collective-permute-done.4.refs_5_ = f32[33,8,128]{2,1,0:T(8,128)S(1)} collective-permute-done((f32[33,8,128]{2,1,0:T(8,128)S(1)}, f32[33,8,128]{2,1,0:T(8,128)S(1)}, u32[]{:S(2)}, u32[]{:S(2)}) %collective-permute-start.4) | collective-permute-done | bytes 135200 | tf_op jit(solution)/shard_map/ppermute | solution.py:431
  115.6 3.9 %collective-permute-done.5.refs_6_ = f32[33,8,128]{2,1,0:T(8,128)S(1)} collective-permute-done((f32[33,8,128]{2,1,0:T(8,128)S(1)}, f32[33,8,128]{2,1,0:T(8,128)S(1)}, u32[]{:S(2)}, u32[]{:S(2)}) %collective-permute-start.5) | collective-permute-done | bytes 135200 | tf_op jit(solution)/shard_map/ppermute | solution.py:431
  119.5 3.8 %collective-permute-done.6.refs_7_ = f32[33,8,128]{2,1,0:T(8,128)S(1)} collective-permute-done((f32[33,8,128]{2,1,0:T(8,128)S(1)}, f32[33,8,128]{2,1,0:T(8,128)S(1)}, u32[]{:S(2)}, u32[]{:S(2)}) %collective-permute-start.6) | collective-permute-done | bytes 135200 | tf_op jit(solution)/shard_map/ppermute | solution.py:431
  123.9 2.4 %regrouped.1 = (f32[8,8,8,128]{3,2,1,0:T(8,128)}, f32[8,8,8,128]{3,2,1,0:T(8,128)}, f32[8,8,8,128]{3,2,1,0:T(8,128)}, f32[8,8,8,128]{3,2,1,0:T(8,128)}, f32[8,8,128]{2,1,0:T(8,128)}) custom-call(f32[33,8,128]{2,1,0:T(8,128)} %get-tuple-element.31.refs_0_, f32[33,8,128]{2,1,0:T(8,128)} %copy-done.3, f32[33,8,128]{2,1,0:T(8,128)} %copy-done.4, ...), custom_call_target="tpu_custom_call" | custom-call | flops 8000000 | bytes 2000000 | tf_op jit(solution)/shard_map/regrouped/pallas_call | solution.py:159
  126.7 4.8 %collective-permute-start.8 = (f32[8,8,8,128]{3,2,1,0:T(8,128)}, f32[8,8,8,128]{3,2,1,0:T(8,128)S(1)}, u32[]{:S(2)}, u32[]{:S(2)}) collective-permute-start(f32[8,8,8,128]{3,2,1,0:T(8,128)} %get-tuple-element.41), channel_id=1, source_target_pairs={{0,2},{1,3},{2,0},{3,1},{4,6},{5,7},{6,4},{7,5},{8,10},{9,11},{10,... | collective-permute-start | bytes 786440 | tf_op jit(solution)/shard_map/ppermute | solution.py:431
  133.7 4.9 %collective-permute-done.10.refs_1_ = f32[8,8,128]{2,1,0:T(8,128)S(1)} collective-permute-done((f32[8,8,128]{2,1,0:T(8,128)}, f32[8,8,128]{2,1,0:T(8,128)S(1)}, u32[]{:S(2)}, u32[]{:S(2)}) %collective-permute-start.10) | collective-permute-done | bytes 32800 | tf_op jit(solution)/shard_map/ppermute | solution.py:431
  138.6 2.3 %collective-permute-start.12 = (f32[8,8,128]{2,1,0:T(8,128)}, f32[8,8,128]{2,1,0:T(8,128)S(1)}, u32[]{:S(2)}, u32[]{:S(2)}) collective-permute-start(f32[8,8,128]{2,1,0:T(8,128)} %get-tuple-element.48.refs_0_), channel_id=1, source_target_pairs={{0,3},{1,0},{2,1},{3,2},{4,7},{5,4},{6,5},{7,6},{8,11},{9,8},{10,9... | collective-permute-start | bytes 98312 | tf_op jit(solution)/shard_map/ppermute | solution.py:431
  141.0 1.4 collective-permute-done.12.refs_3_
  144.3 20.3 %all_gather.3.held = bf16[64,2048]{1,0:T(8,128)(2,1)S(1)} all-gather(bf16[8,2048]{1,0:T(8,128)(2,1)S(1)} %router_rows.1), channel_id=1, replica_groups=mesh['expert'=8,'shard'=32] {'expert'}, dimensions={0}, use_global_device_ids=true | all-gather | bytes 294912 | tf_op jit(solution)/shard_map/all_gather | solution.py:455
  166.2 1.8 %finished.1 = (bf16[64,2048]{1,0:T(8,128)(2,1)S(1)}, bf16[64,2048]{1,0:T(8,128)(2,1)S(1)}) custom-call(f32[8,8,8,128]{3,2,1,0:T(8,128)} %get-tuple-element.39.refs_0_, f32[8,8,8,128]{3,2,1,0:T(8,128)} %copy-done, f32[8,8,8,128]{3,2,1,0:T(8,128)} %copy-done.1, f32[8,8,8,128]{3,2,1,0:T(8,128)} %copy-done.2, f32[8,128]{1,0:T(8,128)S(1)} %get-tuple-element.43.refs_4_), custom_call_target="tpu_custom_call" | custom-call | flops 8000000 | bytes 3000000 | tf_op jit(solution)/shard_map/finished/pallas_call | solution.py:239
  168.7 1.7 %placed.1 = (bf16[352,2048]{1,0:T(8,128)(2,1)}, bf16[352,2048]{1,0:T(8,128)(2,1)}) custom-call(bf16[32,288,128]{2,1,0:T(8,128)(2,1)S(1)} %bitcast.10, bf16[64,2048]{1,0:T(8,128)(2,1)S(1)} %get-tuple-element.44.raw_gate, bf16[64,2048]{1,0:T(8,128)(2,1)S(1)} %get-tuple-element.45.raw_up), custom_call_target="tpu_custom_call" | custom-call | flops 4000000 | bytes 6000000 | tf_op jit(solution)/shard_map/placed/pallas_call | solution.py:355
  (58 shorter events, 10.2 us)
Async XLA Ops:
  42.9 8.1 %copy-start.18 = (f32[33,8,128]{2,1,0:T(8,128)S(1)}, f32[33,8,128]{2,1,0:T(8,128)}, u32[]{:S(2)}) copy-start(f32[33,8,128]{2,1,0:T(8,128)} %get-tuple-element.33) | copy-start | bytes 405508
  42.9 8.4 %copy-start.17 = (f32[33,8,128]{2,1,0:T(8,128)S(1)}, f32[33,8,128]{2,1,0:T(8,128)}, u32[]{:S(2)}) copy-start(f32[33,8,128]{2,1,0:T(8,128)} %get-tuple-element.34) | copy-start | bytes 405508
  42.9 11.8 %copy-start.16 = (f32[33,8,128]{2,1,0:T(8,128)S(1)}, f32[33,8,128]{2,1,0:T(8,128)}, u32[]{:S(2)}) copy-start(f32[33,8,128]{2,1,0:T(8,128)} %get-tuple-element.35) | copy-start | bytes 405508
  43.0 12.8 %copy-start.15 = (f32[33,8,128]{2,1,0:T(8,128)S(1)}, f32[33,8,128]{2,1,0:T(8,128)}, u32[]{:S(2)}) copy-start(f32[33,8,128]{2,1,0:T(8,128)} %get-tuple-element.36) | copy-start | bytes 405508
  43.0 63.3 %copy-start.14 = (f32[33,8,128]{2,1,0:T(8,128)S(1)}, f32[33,8,128]{2,1,0:T(8,128)}, u32[]{:S(2)}) copy-start(f32[33,8,128]{2,1,0:T(8,128)} %get-tuple-element.37) | copy-start | bytes 405508
  43.0 63.3 %copy-start.13 = (f32[33,8,128]{2,1,0:T(8,128)S(1)}, f32[33,8,128]{2,1,0:T(8,128)}, u32[]{:S(2)}) copy-start(f32[33,8,128]{2,1,0:T(8,128)} %get-tuple-element.38) | copy-start | bytes 405508
  43.0 125.7 %all-to-all-start.3 = ((bf16[32,36,8,128]{3,2,1,0:T(8,128)(2,1)}), bf16[32,36,8,128]{3,2,1,0:T(8,128)(2,1)S(1)}, u32[]{:S(2)}, u32[]{:S(2)}) async-start(bf16[32,36,8,128]{3,2,1,0:T(8,128)(2,1)} %packed.1), calls=%async_computation.3 | async-start | bytes 4718592 | tf_op jit(solution)/shard_map/all_to_all | solution.py:422
  49.8 56.5 %collective-permute-start = (f32[33,8,128]{2,1,0:T(8,128)S(1)}, f32[33,8,128]{2,1,0:T(8,128)S(1)}, u32[]{:S(2)}, u32[]{:S(2)}) collective-permute-start(f32[33,8,128]{2,1,0:T(8,128)S(1)} %copy-done.19), channel_id=1, source_target_pairs={{0,4},{1,5},{2,6},{3,7},{4,8},{5,9},{6,10},{7,11},{8,12},{9,13},{1... | collective-permute-start | bytes 405512 | tf_op jit(solution)/shard_map/ppermute | solution.py:431
  51.1 55.2 %collective-permute-start.1 = (f32[33,8,128]{2,1,0:T(8,128)S(1)}, f32[33,8,128]{2,1,0:T(8,128)S(1)}, u32[]{:S(2)}, u32[]{:S(2)}) collective-permute-start(f32[33,8,128]{2,1,0:T(8,128)S(1)} %copy-done.18), channel_id=1, source_target_pairs={{0,28},{1,29},{2,30},{3,31},{4,0},{5,1},{6,2},{7,3},{8,4},{9,5},{1... | collective-permute-start | bytes 405512 | tf_op jit(solution)/shard_map/ppermute | solution.py:431
  51.3 59.0 %collective-permute-start.2 = (f32[33,8,128]{2,1,0:T(8,128)S(1)}, f32[33,8,128]{2,1,0:T(8,128)S(1)}, u32[]{:S(2)}, u32[]{:S(2)}) collective-permute-start(f32[33,8,128]{2,1,0:T(8,128)S(1)} %copy-done.17), channel_id=1, source_target_pairs={{0,16},{1,17},{2,18},{3,19},{4,20},{5,21},{6,22},{7,23},{8,24},{9,... | collective-permute-start | bytes 405512 | tf_op jit(solution)/shard_map/ppermute | solution.py:431
  54.7 58.5 %collective-permute-start.3 = (f32[33,8,128]{2,1,0:T(8,128)S(1)}, f32[33,8,128]{2,1,0:T(8,128)S(1)}, u32[]{:S(2)}, u32[]{:S(2)}) collective-permute-start(f32[33,8,128]{2,1,0:T(8,128)S(1)} %copy-done.16), channel_id=1, source_target_pairs={{0,12},{1,13},{2,14},{3,15},{4,16},{5,17},{6,18},{7,19},{8,20},{9,... | collective-permute-start | bytes 405512 | tf_op jit(solution)/shard_map/ppermute | solution.py:431
  55.8 59.8 %collective-permute-start.4 = (f32[33,8,128]{2,1,0:T(8,128)S(1)}, f32[33,8,128]{2,1,0:T(8,128)S(1)}, u32[]{:S(2)}, u32[]{:S(2)}) collective-permute-start(f32[33,8,128]{2,1,0:T(8,128)S(1)} %copy-done.15), channel_id=1, source_target_pairs={{0,20},{1,21},{2,22},{3,23},{4,24},{5,25},{6,26},{7,27},{8,28},{9,... | collective-permute-start | bytes 405512 | tf_op jit(solution)/shard_map/ppermute | solution.py:431
  106.3 17.0 %copy-start.3 = (f32[33,8,128]{2,1,0:T(8,128)}, f32[33,8,128]{2,1,0:T(8,128)S(1)}, u32[]{:S(2)}) copy-start(f32[33,8,128]{2,1,0:T(8,128)S(1)} %collective-permute-done.refs_1_) | copy-start | bytes 405508
  106.3 13.2 %collective-permute-start.5 = (f32[33,8,128]{2,1,0:T(8,128)S(1)}, f32[33,8,128]{2,1,0:T(8,128)S(1)}, u32[]{:S(2)}, u32[]{:S(2)}) collective-permute-start(f32[33,8,128]{2,1,0:T(8,128)S(1)} %copy-done.14), channel_id=1, source_target_pairs={{0,8},{1,9},{2,10},{3,11},{4,12},{5,13},{6,14},{7,15},{8,16},{9,17... | collective-permute-start | bytes 405512 | tf_op jit(solution)/shard_map/ppermute | solution.py:431
  106.3 16.9 %copy-start.4 = (f32[33,8,128]{2,1,0:T(8,128)}, f32[33,8,128]{2,1,0:T(8,128)S(1)}, u32[]{:S(2)}) copy-start(f32[33,8,128]{2,1,0:T(8,128)S(1)} %collective-permute-done.1.refs_2_) | copy-start | bytes 405508
  106.3 16.9 %collective-permute-start.6 = (f32[33,8,128]{2,1,0:T(8,128)S(1)}, f32[33,8,128]{2,1,0:T(8,128)S(1)}, u32[]{:S(2)}, u32[]{:S(2)}) collective-permute-start(f32[33,8,128]{2,1,0:T(8,128)S(1)} %copy-done.13), channel_id=1, source_target_pairs={{0,24},{1,25},{2,26},{3,27},{4,28},{5,29},{6,30},{7,31},{8,0},{9,1... | collective-permute-start | bytes 405512 | tf_op jit(solution)/shard_map/ppermute | solution.py:431
  110.3 12.9 %copy-start.5 = (f32[33,8,128]{2,1,0:T(8,128)}, f32[33,8,128]{2,1,0:T(8,128)S(1)}, u32[]{:S(2)}) copy-start(f32[33,8,128]{2,1,0:T(8,128)S(1)} %collective-permute-done.2.refs_3_) | copy-start | bytes 405508
  113.3 10.0 %copy-start.6 = (f32[33,8,128]{2,1,0:T(8,128)}, f32[33,8,128]{2,1,0:T(8,128)S(1)}, u32[]{:S(2)}) copy-start(f32[33,8,128]{2,1,0:T(8,128)S(1)} %collective-permute-done.3.refs_4_) | copy-start | bytes 405508
  126.3 39.0 %collective-permute-start.7 = (f32[8,8,8,128]{3,2,1,0:T(8,128)}, f32[8,8,8,128]{3,2,1,0:T(8,128)S(1)}, u32[]{:S(2)}, u32[]{:S(2)}) collective-permute-start(f32[8,8,8,128]{3,2,1,0:T(8,128)} %get-tuple-element.40), channel_id=1, source_target_pairs={{0,1},{1,2},{2,3},{3,0},{4,5},{5,6},{6,7},{7,4},{8,9},{9,10},{10,1... | collective-permute-start | bytes 786440 | tf_op jit(solution)/shard_map/ppermute | solution.py:431
  126.7 38.7 %collective-permute-start.8 = (f32[8,8,8,128]{3,2,1,0:T(8,128)}, f32[8,8,8,128]{3,2,1,0:T(8,128)S(1)}, u32[]{:S(2)}, u32[]{:S(2)}) collective-permute-start(f32[8,8,8,128]{3,2,1,0:T(8,128)} %get-tuple-element.41), channel_id=1, source_target_pairs={{0,2},{1,3},{2,0},{3,1},{4,6},{5,7},{6,4},{7,5},{8,10},{9,11},{10,... | collective-permute-start | bytes 786440 | tf_op jit(solution)/shard_map/ppermute | solution.py:431
  131.5 33.9 %collective-permute-start.9 = (f32[8,8,8,128]{3,2,1,0:T(8,128)}, f32[8,8,8,128]{3,2,1,0:T(8,128)S(1)}, u32[]{:S(2)}, u32[]{:S(2)}) collective-permute-start(f32[8,8,8,128]{3,2,1,0:T(8,128)} %get-tuple-element.42), channel_id=1, source_target_pairs={{0,3},{1,0},{2,1},{3,2},{4,7},{5,4},{6,5},{7,6},{8,11},{9,8},{10,9... | collective-permute-start | bytes 786440 | tf_op jit(solution)/shard_map/ppermute | solution.py:431
  132.5 6.1 %collective-permute-start.10 = (f32[8,8,128]{2,1,0:T(8,128)}, f32[8,8,128]{2,1,0:T(8,128)S(1)}, u32[]{:S(2)}, u32[]{:S(2)}) collective-permute-start(f32[8,8,128]{2,1,0:T(8,128)} %get-tuple-element.48.refs_0_), channel_id=1, source_target_pairs={{0,1},{1,2},{2,3},{3,0},{4,5},{5,6},{6,7},{7,4},{8,9},{9,10},{10,1... | collective-permute-start | bytes 98312 | tf_op jit(solution)/shard_map/ppermute | solution.py:431
  133.0 8.1 %collective-permute-start.11 = (f32[8,8,128]{2,1,0:T(8,128)}, f32[8,8,128]{2,1,0:T(8,128)S(1)}, u32[]{:S(2)}, u32[]{:S(2)}) collective-permute-start(f32[8,8,128]{2,1,0:T(8,128)} %get-tuple-element.48.refs_0_), channel_id=1, source_target_pairs={{0,2},{1,3},{2,0},{3,1},{4,6},{5,7},{6,4},{7,5},{8,10},{9,11},{10,... | collective-permute-start | bytes 98312 | tf_op jit(solution)/shard_map/ppermute | solution.py:431
  138.6 3.9 %collective-permute-start.12 = (f32[8,8,128]{2,1,0:T(8,128)}, f32[8,8,128]{2,1,0:T(8,128)S(1)}, u32[]{:S(2)}, u32[]{:S(2)}) collective-permute-start(f32[8,8,128]{2,1,0:T(8,128)} %get-tuple-element.48.refs_0_), channel_id=1, source_target_pairs={{0,3},{1,0},{2,1},{3,2},{4,7},{5,4},{6,5},{7,6},{8,11},{9,8},{10,9... | collective-permute-start | bytes 98312 | tf_op jit(solution)/shard_map/ppermute | solution.py:431
  (10 other events, 27.2 us)

commit v4 on v3

--- a/solution.py
+++ b/solution.py
@@ -68,10 +68,13 @@
                 totals.append(jnp.sum(jnp.abs(part[e]), axis=0, keepdims=True))
             rows[t].append(jnp.concatenate(totals, axis=1))
     gate_sums, up_sums = (jnp.concatenate(r, axis=0) for r in rows)
-    spare = jnp.zeros((experts, HALF - own), jnp.float32)
-    for d in range(Y * Z):
-        mine = slice(d * own, (d + 1) * own)
-        sums[d % Y, d // Y] = jnp.concatenate([gate_sums[:, mine], spare, up_sums[:, mine], spare], axis=1)
+    spare = [jnp.ones((experts, sums.shape[2] - 2 * own * Z), jnp.float32)]
+    for y in range(Y):
+        parts = []
+        for z in range(Z):
+            mine = slice((z * Y + y) * own, (z * Y + y + 1) * own)
+            parts += [gate_sums[:, mine], up_sums[:, mine]]
+        sums[y] = jnp.concatenate(parts + spare, axis=1)
     copies = [pltpu.make_async_copy(sums, out, sums_sem)]
     copies[0].start()
     for copy in small:
@@ -105,7 +108,7 @@
 def opened(w_gate, w_up, router_weight, router_gain):
     experts, rows, width = w_gate.shape
     router, gain = router_weight.T, router_gain[None]
-    shape = (Y, Z, experts, LANES)
+    shape = (Y, experts, pl.cdiv(2 * width // Y, LANES) * LANES)
     block = (Y * RAW + 1, experts, LANES)
     head = pltpu.VMEM((experts, rows, HEAD), jnp.float32)
     tail = pltpu.VMEM((experts, rows, width - HEAD), jnp.float32)
@@ -219,7 +222,7 @@
     for copy in copies:
         copy.start()
     inverse = 1.0 / scale[...]
-    rows = inverse.shape[0]
+    rows, own = inverse.shape[0], inverse.shape[1] // 2
     for copy in copies:
         copy.wait()
     for p in range(Y * Z // 2):
@@ -227,8 +230,8 @@
         for j in range(RAW):
             first, second = held[2 * p, j], held[2 * p + 1, j]
             place = slice(j * rows, (j + 1) * rows)
-            for out, low in ((gate, 0), (up, HALF)):
-                factor = jnp.broadcast_to(inverse[:, low + j : low + j + 1], (rows, LANES))
+            for out, low, column in ((gate, 0, j), (up, HALF, own + j)):
+                factor = jnp.broadcast_to(inverse[:, column : column + 1], (rows, LANES))
                 both = jnp.concatenate([first[:, low : low + HALF], second[:, low : low + HALF]], axis=1)
                 out[place, lanes] = (both * factor).astype(jnp.bfloat16)
 
@@ -265,9 +268,11 @@
         for copy in pair:
             copy.start()
     own = width // size
-    tiles = [scales[d % Y, d // Y] for d in range(size)]
-    gate_inverse = 1.0 / jnp.concatenate([t[:, :own] for t in tiles], axis=1)
-    up_inverse = 1.0 / jnp.concatenate([t[:, HALF : HALF + own] for t in tiles], axis=1)
+    parts = [
+        [scales[d % Y, :, (d // Y * 2 + t) * own : (d // Y * 2 + t + 1) * own] for d in range(size)]
+        for t in range(2)
+    ]
+    gate_inverse, up_inverse = (1.0 / jnp.concatenate(p, axis=1) for p in parts)
     copies = []
     for c in range(width // LANES):
         columns = slice(c * LANES, (c + 1) * LANES)
@@ -396,7 +401,7 @@
     for copy in copies:
         copy.start()
     for ref in mine:
-        ref[...] = held[lax.axis_index("shard") // Y]
+        ref[...] = held[...]
     for copy in copies:
         copy.wait()
 
@@ -409,7 +414,7 @@
         out_specs=[IN_HBM, IN_VMEM][: 1 + mine],
         out_shape=[
             pltpu.HBM((count, *shape), jnp.float32),
-            pltpu.VMEM(shape[1:], jnp.float32),
+            pltpu.VMEM(shape, jnp.float32),
         ][: 1 + mine],
         scratch_shapes=[pltpu.VMEM(shape, jnp.float32), pltpu.SemaphoreType.DMA((count,))],
         compiler_params=pltpu.CompilerParams(vmem_limit_bytes=1 << 20),
@@ -442,6 +447,9 @@
         if k:
             moved.append(shifted(blocks[k], shift, 0))
     scales, scale = summed(sums, Y, 1.0 / D_MODEL, mine=True)
+    scale = lax.dynamic_slice_in_dim(
+        scale, lax.axis_index("shard") // Y * 2 * own, 2 * own, axis=1
+    )
     scales = exchanged(scales, ALONG_Y)
     serve = packed(w_gate, w_up, *heads, scales)
     serve = exchanged(serve)
@@ -460,7 +468,7 @@
         jnp.transpose(serve_gate, (1, 2, 0)),
         jnp.transpose(serve_up, (1, 2, 0)),
         scale[:, :own],
-        scale[:, HALF : HALF + own],
+        scale[:, own:],
         router.T,
     )
 

time: 171 us -> 168 us (0.982)
  the two profiles are of different devices: /device:TPU:65 before, /device:TPU:8 now
where the time goes in v4:
time: 168 us; the launch traced here: 166 us
  waiting for transfers between devices  61.5 us (37%)
  blocking collectives  49.8 us (30%)
  starting transfers between devices  31.6 us (19%)
  Pallas kernels  18.7 us (11%)
  local copies, waits for them, and re-layouts  3.29 us (2%)
    ppermute x13, waiting for transfers between devices, shifted(): return lax.ppermute(x, 'shard', pairs)  61.5 us
    all_to_all x3, blocking collectives, exchanged(): lax.all_to_all(parts, 'shard', split_axis=0, concat_axis=0, tiled=True, a...  36.6 us
    ppermute x13, starting transfers between devices, shifted(): return lax.ppermute(x, 'shard', pairs)  26.3 us
    all_gather x1, blocking collectives, on_device(): router = lax.all_gather(rows, 'expert', axis=0, tiled=True)  13.2 us
    pallas_call x1, Pallas kernels, opened(): pl.pallas_call(opened_kernel, in_specs=[IN_HBM] * 4, out_specs=[IN_HBM, I...  5.78 us
    all_to_all x1, starting transfers between devices, exchanged(): lax.all_to_all(parts, 'shard', split_axis=0, concat_axis=0, tiled=True, a...  5.31 us
    pallas_call x1, Pallas kernels, packed(): pl.pallas_call(packed_kernel, in_specs=[IN_HBM] * 2 + [IN_VMEM] * 3, out_...  3.7 us
  transfers between devices with their start and end apart: 14, of which 7 were waited for; matrix products, arithmetic and copies ran while one was open for 0% of the time, Pallas kernels for 4%

profile of v4, /device:TPU:8, one launch (start us, length us, event | category | flops | bytes accessed | tf_op | source)
XLA Modules:
  0.0 165.9 jit_solution(2219170084058381458)
XLA Ops:
  0.6 5.8 %opened.1 = (f32[4,8,768]{2,1,0:T(8,128)}, f32[8,64,768]{2,1,0:T(8,128)S(1)}, f32[8,64,768]{2,1,0:T(8,128)S(1)}, f32[33,8,128]{2,1,0:T(8,128)}, f32[33,8,128]{2,...) custom-call(f32[8,64,1408]{2,1,0:T(8,128)} %gate.3, ...), custom_call_target="tpu_custom_call" | custom-call | flops 8000000 | bytes 8000000 | tf_op jit(solution)/shard_map/opened/pallas_call | solution.py:115
  6.4 9.8 %all_to_all.20.arrived = f32[4,8,768]{2,1,0:T(8,128)S(1)} all-to-all(f32[4,8,768]{2,1,0:T(8,128)} %get-tuple-element.29), channel_id=1, replica_groups={{0,1,2,3},{4,5,6,7},{8,9,10,11},{12,13,14,15},{16,17,18,19},{20,21,22,2..., dimensions={0} | all-to-all | bytes 196608 | tf_op jit(solution)/shard_map/all_to_all | solution.py:427
  17.0 17.7 %all_to_all.21.arrived = f32[8,8,768]{2,1,0:T(8,128)S(1)} all-to-all(f32[8,8,768]{2,1,0:T(8,128)} %summed.2), channel_id=1, replica_groups={{0,4,8,12,16,20,24,28},{1,5,9,13,17,21,25,29},{2,6,10,14,18,22,26,30},{..., dimensions={0} | all-to-all | bytes 393216 | tf_op jit(solution)/shard_map/all_to_all | solution.py:427
  35.4 9.1 %all_to_all.22.scales = f32[4,8,768]{2,1,0:T(8,128)S(1)} all-to-all(f32[4,8,768]{2,1,0:T(8,128)} %get-tuple-element.30), channel_id=1, replica_groups={{0,1,2,3},{4,5,6,7},{8,9,10,11},{12,13,14,15},{16,17,18,19},{20,21,22,2..., dimensions={0} | all-to-all | bytes 196608 | tf_op jit(solution)/shard_map/all_to_all | solution.py:427
  44.5 3.7 %packed.1 = bf16[32,36,8,128]{3,2,1,0:T(8,128)(2,1)} custom-call(f32[8,64,1408]{2,1,0:T(8,128)} %gate.3, f32[8,64,1408]{2,1,0:T(8,128)} %up.3, f32[8,64,768]{2,1,0:T(8,128)S(1)} %get-tuple-element.27.gate_head, f32[8,64,768]{2,1,0:T(8,128)S(1)} %get-tuple-element.28.up_head, f32[4,8,768]{2,1,0:T(8,128)S(1)} %all_to_all.22.scales), custom_call_target="tpu_custom_call" | custom-call | flops 8000000 | bytes 9000000 | tf_op jit(solution)/shard_map/packed/pallas_call | solution.py:310
  48.2 5.3 %all-to-all-start.3 = ((bf16[32,36,8,128]{3,2,1,0:T(8,128)(2,1)}), bf16[32,36,8,128]{3,2,1,0:T(8,128)(2,1)S(1)}, u32[]{:S(2)}, u32[]{:S(2)}) async-start(bf16[32,36,8,128]{3,2,1,0:T(8,128)(2,1)} %packed.1), calls=%async_computation.3 | async-start | bytes 4718592 | tf_op jit(solution)/shard_map/all_to_all | solution.py:427
  53.6 1.6 collective-permute-start
  55.1 1.7 %collective-permute-start.1 = (f32[33,8,128]{2,1,0:T(8,128)S(1)}, f32[33,8,128]{2,1,0:T(8,128)S(1)}, u32[]{:S(2)}, u32[]{:S(2)}) collective-permute-start(f32[33,8,128]{2,1,0:T(8,128)S(1)} %copy-done.18), channel_id=1, source_target_pairs={{0,28},{1,29},{2,30},{3,31},{4,0},{5,1},{6,2},{7,3},{8,4},{9,5},{1... | collective-permute-start | bytes 405512 | tf_op jit(solution)/shard_map/ppermute | solution.py:436
  56.9 5.5 %collective-permute-start.2 = (f32[33,8,128]{2,1,0:T(8,128)S(1)}, f32[33,8,128]{2,1,0:T(8,128)S(1)}, u32[]{:S(2)}, u32[]{:S(2)}) collective-permute-start(f32[33,8,128]{2,1,0:T(8,128)S(1)} %copy-done.17), channel_id=1, source_target_pairs={{0,16},{1,17},{2,18},{3,19},{4,20},{5,21},{6,22},{7,23},{8,24},{9,... | collective-permute-start | bytes 405512 | tf_op jit(solution)/shard_map/ppermute | solution.py:436
  62.4 5.0 %collective-permute-start.4 = (f32[33,8,128]{2,1,0:T(8,128)S(1)}, f32[33,8,128]{2,1,0:T(8,128)S(1)}, u32[]{:S(2)}, u32[]{:S(2)}) collective-permute-start(f32[33,8,128]{2,1,0:T(8,128)S(1)} %copy-done.15), channel_id=1, source_target_pairs={{0,20},{1,21},{2,22},{3,23},{4,24},{5,25},{6,26},{7,27},{8,28},{9,... | collective-permute-start | bytes 405512 | tf_op jit(solution)/shard_map/ppermute | solution.py:436
  67.4 48.3 %collective-permute-done.refs_1_ = f32[33,8,128]{2,1,0:T(8,128)S(1)} collective-permute-done((f32[33,8,128]{2,1,0:T(8,128)S(1)}, f32[33,8,128]{2,1,0:T(8,128)S(1)}, u32[]{:S(2)}, u32[]{:S(2)}) %collective-permute-start) | collective-permute-done | bytes 135200 | tf_op jit(solution)/shard_map/ppermute | solution.py:436
  116.3 3.6 %collective-permute-start.6 = (f32[33,8,128]{2,1,0:T(8,128)S(1)}, f32[33,8,128]{2,1,0:T(8,128)S(1)}, u32[]{:S(2)}, u32[]{:S(2)}) collective-permute-start(f32[33,8,128]{2,1,0:T(8,128)S(1)} %copy-done.13), channel_id=1, source_target_pairs={{0,24},{1,25},{2,26},{3,27},{4,28},{5,29},{6,30},{7,31},{8,0},{9,1... | collective-permute-start | bytes 405512 | tf_op jit(solution)/shard_map/ppermute | solution.py:436
  120.3 3.9 %collective-permute-done.3.refs_4_ = f32[33,8,128]{2,1,0:T(8,128)S(1)} collective-permute-done((f32[33,8,128]{2,1,0:T(8,128)S(1)}, f32[33,8,128]{2,1,0:T(8,128)S(1)}, u32[]{:S(2)}, u32[]{:S(2)}) %collective-permute-start.3) | collective-permute-done | bytes 135200 | tf_op jit(solution)/shard_map/ppermute | solution.py:436
  124.2 2.9 %collective-permute-done.5.refs_6_ = f32[33,8,128]{2,1,0:T(8,128)S(1)} collective-permute-done((f32[33,8,128]{2,1,0:T(8,128)S(1)}, f32[33,8,128]{2,1,0:T(8,128)S(1)}, u32[]{:S(2)}, u32[]{:S(2)}) %collective-permute-start.5) | collective-permute-done | bytes 135200 | tf_op jit(solution)/shard_map/ppermute | solution.py:436
  127.9 2.4 %regrouped.1 = (f32[8,8,8,128]{3,2,1,0:T(8,128)}, f32[8,8,8,128]{3,2,1,0:T(8,128)}, f32[8,8,8,128]{3,2,1,0:T(8,128)}, f32[8,8,8,128]{3,2,1,0:T(8,128)}, f32[8,8,128]{2,1,0:T(8,128)}) custom-call(f32[33,8,128]{2,1,0:T(8,128)} %get-tuple-element.31.refs_0_, f32[33,8,128]{2,1,0:T(8,128)} %copy-done.3, f32[33,8,128]{2,1,0:T(8,128)} %copy-done.4, ...), custom_call_target="tpu_custom_call" | custom-call | flops 8000000 | bytes 2000000 | tf_op jit(solution)/shard_map/regrouped/pallas_call | solution.py:162
  130.3 1.8 %collective-permute-start.10 = (f32[8,8,128]{2,1,0:T(8,128)}, f32[8,8,128]{2,1,0:T(8,128)S(1)}, u32[]{:S(2)}, u32[]{:S(2)}) collective-permute-start(f32[8,8,128]{2,1,0:T(8,128)} %get-tuple-element.48.refs_0_), channel_id=1, source_target_pairs={{0,1},{1,2},{2,3},{3,0},{4,5},{5,6},{6,7},{7,4},{8,9},{9,10},{10,1... | collective-permute-start | bytes 98312 | tf_op jit(solution)/shard_map/ppermute | solution.py:436
  132.9 1.6 collective-permute-start.8
  134.4 1.9 %collective-permute-start.9 = (f32[8,8,8,128]{3,2,1,0:T(8,128)}, f32[8,8,8,128]{3,2,1,0:T(8,128)S(1)}, u32[]{:S(2)}, u32[]{:S(2)}) collective-permute-start(f32[8,8,8,128]{3,2,1,0:T(8,128)} %get-tuple-element.42), channel_id=1, source_target_pairs={{0,3},{1,0},{2,1},{3,2},{4,7},{5,4},{6,5},{7,6},{8,11},{9,8},{10,9... | collective-permute-start | bytes 786440 | tf_op jit(solution)/shard_map/ppermute | solution.py:436
  137.0 1.5 collective-permute-start.12
  138.5 5.7 %collective-permute-done.11.refs_2_ = f32[8,8,128]{2,1,0:T(8,128)S(1)} collective-permute-done((f32[8,8,128]{2,1,0:T(8,128)}, f32[8,8,128]{2,1,0:T(8,128)S(1)}, u32[]{:S(2)}, u32[]{:S(2)}) %collective-permute-start.11) | collective-permute-done | bytes 32800 | tf_op jit(solution)/shard_map/ppermute | solution.py:436
  145.5 1.2 router_rows.1
  146.7 13.2 %all_gather.3.held = bf16[64,2048]{1,0:T(8,128)(2,1)S(1)} all-gather(bf16[8,2048]{1,0:T(8,128)(2,1)S(1)} %router_rows.1), channel_id=1, replica_groups=mesh['expert'=8,'shard'=32] {'expert'}, dimensions={0}, use_global_device_ids=true | all-gather | bytes 294912 | tf_op jit(solution)/shard_map/all_gather | solution.py:463
  161.5 1.8 %finished.1 = (bf16[64,2048]{1,0:T(8,128)(2,1)S(1)}, bf16[64,2048]{1,0:T(8,128)(2,1)S(1)}) custom-call(f32[8,8,8,128]{3,2,1,0:T(8,128)} %get-tuple-element.39.refs_0_, f32[8,8,8,128]{3,2,1,0:T(8,128)} %copy-done, f32[8,8,8,128]{3,2,1,0:T(8,128)} %copy-done.1, f32[8,8,8,128]{3,2,1,0:T(8,128)} %copy-done.2, f32[8,88]{1,0:T(8,128)S(1)} %constant_dynamic-slice_fusion.refs_4_), custom_call_target="tpu_custom_call" | custom-call | flops 8000000 | bytes 3000000 | tf_op jit(solution)/shard_map/finished/pallas_call | solution.py:242
  164.0 1.7 %placed.1 = (bf16[352,2048]{1,0:T(8,128)(2,1)}, bf16[352,2048]{1,0:T(8,128)(2,1)}) custom-call(bf16[32,288,128]{2,1,0:T(8,128)(2,1)S(1)} %bitcast.10, bf16[64,2048]{1,0:T(8,128)(2,1)S(1)} %get-tuple-element.44.raw_gate, bf16[64,2048]{1,0:T(8,128)(2,1)S(1)} %get-tuple-element.45.raw_up), custom_call_target="tpu_custom_call" | custom-call | flops 4000000 | bytes 6000000 | tf_op jit(solution)/shard_map/placed/pallas_call | solution.py:360
  (59 shorter events, 8.2 us)
Async XLA Ops:
  48.2 7.0 %copy-start.18 = (f32[33,8,128]{2,1,0:T(8,128)S(1)}, f32[33,8,128]{2,1,0:T(8,128)}, u32[]{:S(2)}) copy-start(f32[33,8,128]{2,1,0:T(8,128)} %get-tuple-element.33) | copy-start | bytes 405508
  48.2 8.7 %copy-start.17 = (f32[33,8,128]{2,1,0:T(8,128)S(1)}, f32[33,8,128]{2,1,0:T(8,128)}, u32[]{:S(2)}) copy-start(f32[33,8,128]{2,1,0:T(8,128)} %get-tuple-element.34) | copy-start | bytes 405508
  48.2 14.2 %copy-start.16 = (f32[33,8,128]{2,1,0:T(8,128)S(1)}, f32[33,8,128]{2,1,0:T(8,128)}, u32[]{:S(2)}) copy-start(f32[33,8,128]{2,1,0:T(8,128)} %get-tuple-element.35) | copy-start | bytes 405508
  48.2 14.2 %copy-start.15 = (f32[33,8,128]{2,1,0:T(8,128)S(1)}, f32[33,8,128]{2,1,0:T(8,128)}, u32[]{:S(2)}) copy-start(f32[33,8,128]{2,1,0:T(8,128)} %get-tuple-element.36) | copy-start | bytes 405508
  48.2 67.5 %copy-start.14 = (f32[33,8,128]{2,1,0:T(8,128)S(1)}, f32[33,8,128]{2,1,0:T(8,128)}, u32[]{:S(2)}) copy-start(f32[33,8,128]{2,1,0:T(8,128)} %get-tuple-element.37) | copy-start | bytes 405508
  48.2 68.1 %copy-start.13 = (f32[33,8,128]{2,1,0:T(8,128)S(1)}, f32[33,8,128]{2,1,0:T(8,128)}, u32[]{:S(2)}) copy-start(f32[33,8,128]{2,1,0:T(8,128)} %get-tuple-element.38) | copy-start | bytes 405508
  48.2 115.8 %all-to-all-start.3 = ((bf16[32,36,8,128]{3,2,1,0:T(8,128)(2,1)}), bf16[32,36,8,128]{3,2,1,0:T(8,128)(2,1)S(1)}, u32[]{:S(2)}, u32[]{:S(2)}) async-start(bf16[32,36,8,128]{3,2,1,0:T(8,128)(2,1)} %packed.1), calls=%async_computation.3 | async-start | bytes 4718592 | tf_op jit(solution)/shard_map/all_to_all | solution.py:427
  53.6 62.1 %collective-permute-start = (f32[33,8,128]{2,1,0:T(8,128)S(1)}, f32[33,8,128]{2,1,0:T(8,128)S(1)}, u32[]{:S(2)}, u32[]{:S(2)}) collective-permute-start(f32[33,8,128]{2,1,0:T(8,128)S(1)} %copy-done.19), channel_id=1, source_target_pairs={{0,4},{1,5},{2,6},{3,7},{4,8},{5,9},{6,10},{7,11},{8,12},{9,13},{1... | collective-permute-start | bytes 405512 | tf_op jit(solution)/shard_map/ppermute | solution.py:436
  55.1 61.2 %collective-permute-start.1 = (f32[33,8,128]{2,1,0:T(8,128)S(1)}, f32[33,8,128]{2,1,0:T(8,128)S(1)}, u32[]{:S(2)}, u32[]{:S(2)}) collective-permute-start(f32[33,8,128]{2,1,0:T(8,128)S(1)} %copy-done.18), channel_id=1, source_target_pairs={{0,28},{1,29},{2,30},{3,31},{4,0},{5,1},{6,2},{7,3},{8,4},{9,5},{1... | collective-permute-start | bytes 405512 | tf_op jit(solution)/shard_map/ppermute | solution.py:436
  56.9 63.4 %collective-permute-start.2 = (f32[33,8,128]{2,1,0:T(8,128)S(1)}, f32[33,8,128]{2,1,0:T(8,128)S(1)}, u32[]{:S(2)}, u32[]{:S(2)}) collective-permute-start(f32[33,8,128]{2,1,0:T(8,128)S(1)} %copy-done.17), channel_id=1, source_target_pairs={{0,16},{1,17},{2,18},{3,19},{4,20},{5,21},{6,22},{7,23},{8,24},{9,... | collective-permute-start | bytes 405512 | tf_op jit(solution)/shard_map/ppermute | solution.py:436
  62.4 61.8 %collective-permute-start.3 = (f32[33,8,128]{2,1,0:T(8,128)S(1)}, f32[33,8,128]{2,1,0:T(8,128)S(1)}, u32[]{:S(2)}, u32[]{:S(2)}) collective-permute-start(f32[33,8,128]{2,1,0:T(8,128)S(1)} %copy-done.16), channel_id=1, source_target_pairs={{0,12},{1,13},{2,14},{3,15},{4,16},{5,17},{6,18},{7,19},{8,20},{9,... | collective-permute-start | bytes 405512 | tf_op jit(solution)/shard_map/ppermute | solution.py:436
  62.4 61.8 %collective-permute-start.4 = (f32[33,8,128]{2,1,0:T(8,128)S(1)}, f32[33,8,128]{2,1,0:T(8,128)S(1)}, u32[]{:S(2)}, u32[]{:S(2)}) collective-permute-start(f32[33,8,128]{2,1,0:T(8,128)S(1)} %copy-done.15), channel_id=1, source_target_pairs={{0,20},{1,21},{2,22},{3,23},{4,24},{5,25},{6,26},{7,27},{8,28},{9,... | collective-permute-start | bytes 405512 | tf_op jit(solution)/shard_map/ppermute | solution.py:436
  115.7 11.6 %copy-start.3 = (f32[33,8,128]{2,1,0:T(8,128)}, f32[33,8,128]{2,1,0:T(8,128)S(1)}, u32[]{:S(2)}) copy-start(f32[33,8,128]{2,1,0:T(8,128)S(1)} %collective-permute-done.refs_1_) | copy-start | bytes 405508
  115.7 11.4 %collective-permute-start.5 = (f32[33,8,128]{2,1,0:T(8,128)S(1)}, f32[33,8,128]{2,1,0:T(8,128)S(1)}, u32[]{:S(2)}, u32[]{:S(2)}) collective-permute-start(f32[33,8,128]{2,1,0:T(8,128)S(1)} %copy-done.14), channel_id=1, source_target_pairs={{0,8},{1,9},{2,10},{3,11},{4,12},{5,13},{6,14},{7,15},{8,16},{9,17... | collective-permute-start | bytes 405512 | tf_op jit(solution)/shard_map/ppermute | solution.py:436
  116.3 10.9 %copy-start.4 = (f32[33,8,128]{2,1,0:T(8,128)}, f32[33,8,128]{2,1,0:T(8,128)S(1)}, u32[]{:S(2)}) copy-start(f32[33,8,128]{2,1,0:T(8,128)S(1)} %collective-permute-done.1.refs_2_) | copy-start | bytes 405508
  116.3 10.9 %collective-permute-start.6 = (f32[33,8,128]{2,1,0:T(8,128)S(1)}, f32[33,8,128]{2,1,0:T(8,128)S(1)}, u32[]{:S(2)}, u32[]{:S(2)}) collective-permute-start(f32[33,8,128]{2,1,0:T(8,128)S(1)} %copy-done.13), channel_id=1, source_target_pairs={{0,24},{1,25},{2,26},{3,27},{4,28},{5,29},{6,30},{7,31},{8,0},{9,1... | collective-permute-start | bytes 405512 | tf_op jit(solution)/shard_map/ppermute | solution.py:436
  120.3 7.0 %copy-start.5 = (f32[33,8,128]{2,1,0:T(8,128)}, f32[33,8,128]{2,1,0:T(8,128)S(1)}, u32[]{:S(2)}) copy-start(f32[33,8,128]{2,1,0:T(8,128)S(1)} %collective-permute-done.2.refs_3_) | copy-start | bytes 405508
  130.3 6.7 %collective-permute-start.10 = (f32[8,8,128]{2,1,0:T(8,128)}, f32[8,8,128]{2,1,0:T(8,128)S(1)}, u32[]{:S(2)}, u32[]{:S(2)}) collective-permute-start(f32[8,8,128]{2,1,0:T(8,128)} %get-tuple-element.48.refs_0_), channel_id=1, source_target_pairs={{0,1},{1,2},{2,3},{3,0},{4,5},{5,6},{6,7},{7,4},{8,9},{9,10},{10,1... | collective-permute-start | bytes 98312 | tf_op jit(solution)/shard_map/ppermute | solution.py:436
  132.0 28.6 %collective-permute-start.7 = (f32[8,8,8,128]{3,2,1,0:T(8,128)}, f32[8,8,8,128]{3,2,1,0:T(8,128)S(1)}, u32[]{:S(2)}, u32[]{:S(2)}) collective-permute-start(f32[8,8,8,128]{3,2,1,0:T(8,128)} %get-tuple-element.40), channel_id=1, source_target_pairs={{0,1},{1,2},{2,3},{3,0},{4,5},{5,6},{6,7},{7,4},{8,9},{9,10},{10,1... | collective-permute-start | bytes 786440 | tf_op jit(solution)/shard_map/ppermute | solution.py:436
  132.9 27.8 %collective-permute-start.8 = (f32[8,8,8,128]{3,2,1,0:T(8,128)}, f32[8,8,8,128]{3,2,1,0:T(8,128)S(1)}, u32[]{:S(2)}, u32[]{:S(2)}) collective-permute-start(f32[8,8,8,128]{3,2,1,0:T(8,128)} %get-tuple-element.41), channel_id=1, source_target_pairs={{0,2},{1,3},{2,0},{3,1},{4,6},{5,7},{6,4},{7,5},{8,10},{9,11},{10,... | collective-permute-start | bytes 786440 | tf_op jit(solution)/shard_map/ppermute | solution.py:436
  134.4 26.2 %collective-permute-start.9 = (f32[8,8,8,128]{3,2,1,0:T(8,128)}, f32[8,8,8,128]{3,2,1,0:T(8,128)S(1)}, u32[]{:S(2)}, u32[]{:S(2)}) collective-permute-start(f32[8,8,8,128]{3,2,1,0:T(8,128)} %get-tuple-element.42), channel_id=1, source_target_pairs={{0,3},{1,0},{2,1},{3,2},{4,7},{5,4},{6,5},{7,6},{8,11},{9,8},{10,9... | collective-permute-start | bytes 786440 | tf_op jit(solution)/shard_map/ppermute | solution.py:436
  136.4 7.9 %collective-permute-start.11 = (f32[8,8,128]{2,1,0:T(8,128)}, f32[8,8,128]{2,1,0:T(8,128)S(1)}, u32[]{:S(2)}, u32[]{:S(2)}) collective-permute-start(f32[8,8,128]{2,1,0:T(8,128)} %get-tuple-element.48.refs_0_), channel_id=1, source_target_pairs={{0,2},{1,3},{2,0},{3,1},{4,6},{5,7},{6,4},{7,5},{8,10},{9,11},{10,... | collective-permute-start | bytes 98312 | tf_op jit(solution)/shard_map/ppermute | solution.py:436
  137.0 7.5 %copy-start.10 = (f32[8,8,128]{2,1,0:T(8,128)}, f32[8,8,128]{2,1,0:T(8,128)S(1)}, u32[]{:S(2)}) copy-start(f32[8,8,128]{2,1,0:T(8,128)S(1)} %collective-permute-done.10.refs_1_) | copy-start | bytes 98308
  137.0 7.5 %collective-permute-start.12 = (f32[8,8,128]{2,1,0:T(8,128)}, f32[8,8,128]{2,1,0:T(8,128)S(1)}, u32[]{:S(2)}, u32[]{:S(2)}) collective-permute-start(f32[8,8,128]{2,1,0:T(8,128)} %get-tuple-element.48.refs_0_), channel_id=1, source_target_pairs={{0,3},{1,0},{2,1},{3,2},{4,7},{5,4},{6,5},{7,6},{8,11},{9,8},{10,9... | collective-permute-start | bytes 98312 | tf_op jit(solution)/shard_map/ppermute | solution.py:436
  (10 other events, 16.5 us)
